TPU v7x, 32 devices: a whole 2x2x4 slice. The times are simulated.
32 devices in a mesh: seq: 8 (over z, core), fsdp: 4 (over y, x).
Axes of the slice: x: 2, y: 2, z: 4, core: 2. Of those that a mesh axis runs over, the one named last changes fastest.
Arguments:
- block_input: bfloat16 [8, 1472, 1152], P('fsdp', 'seq')
- key_mask: int32 [16, 736], P('fsdp'), may hold values from 0 to 1, as said below
- slot_flags: int32 [16], P('fsdp'), may hold values from 0 to 1, as said below
- norm1_gain: bfloat16 [1152], P('fsdp'), may hold values from 0.5 to 1.5
- norm1_bias: bfloat16 [1152], P('fsdp'), may hold values from -3 to 3
- qkv_weight: bfloat16 [1152, 3456], P('fsdp'), may hold values from -0.25 to 0.25
- query_bias: bfloat16 [1152], P('fsdp'), may hold values from -3 to 3
- value_bias: bfloat16 [1152], P('fsdp'), may hold values from -3 to 3
- proj_weight: bfloat16 [1152, 1152], P('fsdp'), may hold values from -0.375 to 0.375
- proj_bias: bfloat16 [1152], P('fsdp'), may hold values from -3 to 3
- norm2_gain: bfloat16 [1152], P('fsdp'), may hold values from 0.5 to 1.5
- norm2_bias: bfloat16 [1152], P('fsdp'), may hold values from -3 to 3
- up_weight: bfloat16 [1152, 4304], P('fsdp'), may hold values from -0.1875 to 0.1875
- up_bias: bfloat16 [4304], P('fsdp'), may hold values from -3 to 3
- down_weight: bfloat16 [4304, 1152], P(None, 'fsdp'), may hold values from -0.09375 to 0.09375
- down_bias: bfloat16 [1152], P('fsdp'), may hold values from -3 to 3
- out_grad: bfloat16 [8, 1472, 1152], P('fsdp', 'seq'), may hold values from -6 to 6
Outputs:
- block_output: bfloat16 [8, 1472, 1152], P('fsdp', 'seq')
- input_grad: float32 [8, 1472, 1152], P('fsdp', 'seq')
- norm1_gain_grad: float32 [1152], P('fsdp')
- norm1_bias_grad: float32 [1152], P('fsdp')
- qkv_weight_grad: float32 [1152, 3456], P('fsdp')
- query_bias_grad: float32 [1152], P('fsdp')
- value_bias_grad: float32 [1152], P('fsdp')
- proj_weight_grad: float32 [1152, 1152], P('fsdp')
- proj_bias_grad: float32 [1152], P('fsdp')
- norm2_gain_grad: float32 [1152], P('fsdp')
- norm2_bias_grad: float32 [1152], P('fsdp')
- up_weight_grad: float32 [1152, 4304], P('fsdp')
- up_bias_grad: float32 [4304], P('fsdp')
- down_weight_grad: float32 [4304, 1152], P(None, 'fsdp')
- down_bias_grad: float32 [1152], P('fsdp')
Inputs may be any that keep to these rules, and one draw needn't show every extreme that they name: `key_mask`: positions 729 and beyond are 0 in every slot; every position of a slot whose flag is 0 is 0. `slot_flags`: exactly max(1, 1) slots have flag 0, at places drawn from the seed.
All inputs are finite; a program needn't handle non-finite values.
Results may differ from a plain program's by a relative error of at most 0.012.
The roundings to bfloat16 on the way count: a program that leaves them out, or rounds other values in their place, can miss the bound.
Values may be sent and summed in bfloat16 or wider, within the bound.
A program may use at most 256 MiB of HBM per device.

v0:
```python
import jax
import jax.numpy as jnp
from jax import lax
from jax.sharding import PartitionSpec as P

HEAD = 72


epsilon = 1e-06


def as_sent(array):
    return jax.tree.map(lambda a: a.astype(jnp.bfloat16) if a.dtype == jnp.float32 else a, array)


def layer_norm(values, gain_vec, bias_vec):
    row_mean = jnp.mean(values, axis=-1, keepdims=True)
    centered = values - row_mean
    variance = jnp.mean(centered * centered, axis=-1, keepdims=True)
    return centered * lax.rsqrt(variance + epsilon) * gain_vec + bias_vec


def gelu_tanh(values):
    return (
        0.5
        * values
        * (1.0 + jnp.tanh(0.7978845608028654 * (values + 0.044715 * values * values * values)))
    )


def masked_scores(queries, key_vecs, key_live):
    score_scale = queries.shape[-1] ** (-0.5)
    scores = (
        jnp.einsum("qhd,khd->hqk", queries, key_vecs, preferred_element_type=jnp.float32)
        * score_scale
    )
    return scores + ((key_live.astype(jnp.float32) - 1.0) * 10000.0)[None, None, :]


def attend_forward(packed):
    queries, key_vecs, value_vecs, key_live = packed
    shifted = masked_scores(queries, key_vecs, key_live)
    row_max = jnp.max(shifted, axis=-1, keepdims=True)
    exp_terms = jnp.exp(shifted - row_max)
    row_total = jnp.sum(exp_terms, axis=-1, keepdims=True)
    weights_low = (exp_terms / row_total).astype(jnp.bfloat16)
    attended = jnp.einsum(
        "hqk,khd->qhd", weights_low, value_vecs, preferred_element_type=jnp.float32
    )
    return (attended.astype(jnp.bfloat16), row_max + jnp.log(row_total))


def attend_backward(packed):
    queries, key_vecs, value_vecs, key_live, log_total, grad_out = packed
    score_scale = queries.shape[-1] ** (-0.5)
    shifted = masked_scores(queries, key_vecs, key_live)
    probabilities = jnp.exp(shifted - log_total)
    weights_low = probabilities.astype(jnp.bfloat16)
    grad_probs = jnp.einsum(
        "qhd,khd->hqk", grad_out, value_vecs, preferred_element_type=jnp.float32
    )
    row_dot = jnp.sum(probabilities * grad_probs, axis=-1, keepdims=True)
    grad_scores = (probabilities * (grad_probs - row_dot)).astype(jnp.bfloat16)
    grad_q = (
        jnp.einsum("hqk,khd->qhd", grad_scores, key_vecs, preferred_element_type=jnp.float32)
        * score_scale
    ).astype(jnp.bfloat16)
    grad_k = (
        jnp.einsum("hqk,qhd->khd", grad_scores, queries, preferred_element_type=jnp.float32)
        * score_scale
    ).astype(jnp.bfloat16)
    grad_v = jnp.einsum(
        "hqk,qhd->khd", weights_low, grad_out, preferred_element_type=jnp.float32
    ).astype(jnp.bfloat16)
    return (grad_q, grad_k, grad_v)


def forward_pass(block_input, key_mask, row_flags, gathered, repeat):
    (
        gain_one,
        bias_one,
        qkv_full,
        query_shift,
        value_shift,
        proj_full,
        proj_shift,
        gain_two,
        bias_two,
        up_full,
        up_shift,
        down_full,
        down_shift,
    ) = gathered
    pair_count, part_rows, model_width = block_input.shape
    token_rows = block_input.reshape(pair_count * part_rows, model_width).astype(jnp.float32)
    normed, norm_one_back = jax.vjp(
        layer_norm, token_rows, gain_one.astype(jnp.float32), bias_one.astype(jnp.float32)
    )
    normed_low = normed.astype(jnp.bfloat16)
    mixed_rows = jnp.dot(normed_low, qkv_full, preferred_element_type=jnp.float32)
    token_shape = (pair_count, part_rows, model_width)
    queries = (
        (mixed_rows[:, :model_width] + query_shift.astype(jnp.float32))
        .astype(jnp.bfloat16)
        .reshape(token_shape)
    )
    key_vecs = (
        mixed_rows[:, model_width : 2 * model_width].astype(jnp.bfloat16).reshape(token_shape)
    )
    value_vecs = (
        (mixed_rows[:, 2 * model_width :] + value_shift.astype(jnp.float32))
        .astype(jnp.bfloat16)
        .reshape(token_shape)
    )
    if repeat:
        head_parts = (
            lax.all_to_all(queries, "seq", split_axis=2, concat_axis=1, tiled=True),
            lax.all_to_all(key_vecs, "seq", split_axis=2, concat_axis=1, tiled=True),
            lax.all_to_all(value_vecs, "seq", split_axis=2, concat_axis=1, tiled=True),
        )
    else:
        head_parts = (
            lax.all_to_all(queries, "seq", split_axis=2, concat_axis=1, tiled=True),
            lax.all_to_all(key_vecs, "seq", split_axis=2, concat_axis=1, tiled=True),
            lax.all_to_all(value_vecs, "seq", split_axis=2, concat_axis=1, tiled=True),
        )
    layout = head_parts[0].shape
    head_shape = (pair_count * 2, layout[1] // 2, layout[2] // HEAD, HEAD)
    split_heads = (
        head_parts[0].reshape(head_shape),
        head_parts[1].reshape(head_shape),
        head_parts[2].reshape(head_shape),
    )
    attended, log_total = lax.map(attend_forward, split_heads + (key_mask,))
    attended = attended.reshape(layout)
    if repeat:
        merged = lax.all_to_all(attended, "seq", split_axis=1, concat_axis=2, tiled=True)
    else:
        merged = lax.all_to_all(attended, "seq", split_axis=1, concat_axis=2, tiled=True)
    merged_rows = merged.reshape(pair_count * part_rows, model_width)
    hidden = (
        token_rows
        + jnp.dot(merged_rows, proj_full, preferred_element_type=jnp.float32)
        + proj_shift.astype(jnp.float32)
    )
    second, norm_two_back = jax.vjp(
        layer_norm, hidden, gain_two.astype(jnp.float32), bias_two.astype(jnp.float32)
    )
    second_low = second.astype(jnp.bfloat16)
    gate_in = jnp.dot(second_low, up_full, preferred_element_type=jnp.float32) + up_shift.astype(
        jnp.float32
    )
    active, gelu_back = jax.vjp(gelu_tanh, gate_in)
    active_low = active.astype(jnp.bfloat16)
    result = (
        hidden
        + jnp.dot(active_low, down_full, preferred_element_type=jnp.float32)
        + down_shift.astype(jnp.float32)
    )
    output = (result.reshape(token_shape) * row_flags[:, None, None]).astype(jnp.bfloat16)
    return dict(
        normed_low=normed_low,
        norm_one_back=norm_one_back,
        split_heads=split_heads,
        log_total=log_total,
        merged_rows=merged_rows,
        norm_two_back=norm_two_back,
        second_low=second_low,
        gelu_back=gelu_back,
        active_low=active_low,
        output=output,
    )


def shards(
    block_input,
    key_mask,
    slot_flags,
    norm1_gain,
    norm1_bias,
    qkv_weight,
    query_bias,
    value_bias,
    proj_weight,
    proj_bias,
    norm2_gain,
    norm2_bias,
    up_weight,
    up_bias,
    down_weight,
    down_bias,
    out_grad,
):
    gathered = (
        lax.all_gather(norm1_gain, "fsdp", axis=0, tiled=True),
        lax.all_gather(norm1_bias, "fsdp", axis=0, tiled=True),
        lax.all_gather(qkv_weight, "fsdp", axis=0, tiled=True),
        lax.all_gather(query_bias, "fsdp", axis=0, tiled=True),
        lax.all_gather(value_bias, "fsdp", axis=0, tiled=True),
        lax.all_gather(proj_weight, "fsdp", axis=0, tiled=True),
        lax.all_gather(proj_bias, "fsdp", axis=0, tiled=True),
        lax.all_gather(norm2_gain, "fsdp", axis=0, tiled=True),
        lax.all_gather(norm2_bias, "fsdp", axis=0, tiled=True),
        lax.all_gather(up_weight, "fsdp", axis=0, tiled=True),
        lax.all_gather(up_bias, "fsdp", axis=0, tiled=True),
        lax.all_gather(down_weight, "fsdp", axis=1, tiled=True),
        lax.all_gather(down_bias, "fsdp", axis=0, tiled=True),
    )
    which_half = lax.axis_index("seq") // (lax.axis_size("seq") // 2)
    flag_pairs = slot_flags.astype(jnp.float32).reshape(-1, 2)
    row_flags = jnp.where(which_half == 0, flag_pairs[:, 0], flag_pairs[:, 1])
    first = forward_pass(block_input, key_mask, row_flags, gathered, False)
    kept_state = forward_pass(block_input, key_mask, row_flags, gathered, True)
    qkv_full = gathered[2]
    proj_full = gathered[5]
    up_full = gathered[9]
    down_full = gathered[11]
    pair_count, part_rows, model_width = block_input.shape
    grad_rows = (out_grad.astype(jnp.float32) * row_flags[:, None, None]).reshape(
        pair_count * part_rows, model_width
    )
    grad_low = grad_rows.astype(jnp.bfloat16)
    down_weight_grad = jnp.einsum(
        "rf,rd->fd", kept_state["active_low"], grad_low, preferred_element_type=jnp.float32
    )
    down_bias_grad = jnp.sum(grad_rows, axis=0)
    grad_active = jnp.einsum("rd,fd->rf", grad_low, down_full, preferred_element_type=jnp.float32)
    grad_gate = kept_state["gelu_back"](grad_active)[0].astype(jnp.bfloat16)
    up_weight_grad = jnp.einsum(
        "rd,rf->df", kept_state["second_low"], grad_gate, preferred_element_type=jnp.float32
    )
    up_bias_grad = jnp.sum(grad_gate.astype(jnp.float32), axis=0)
    grad_second = jnp.einsum("rf,df->rd", grad_gate, up_full, preferred_element_type=jnp.float32)
    grad_hidden_norm, norm2_gain_grad, norm2_bias_grad = kept_state["norm_two_back"](grad_second)
    grad_hidden = grad_rows + grad_hidden_norm
    grad_branch = grad_hidden.astype(jnp.bfloat16)
    proj_weight_grad = jnp.einsum(
        "ri,ro->io", kept_state["merged_rows"], grad_branch, preferred_element_type=jnp.float32
    )
    proj_bias_grad = jnp.sum(grad_branch.astype(jnp.float32), axis=0)
    grad_merged = jnp.einsum(
        "ro,io->ri", grad_branch, proj_full, preferred_element_type=jnp.float32
    ).astype(jnp.bfloat16)
    grad_heads = lax.all_to_all(
        grad_merged.reshape(pair_count, part_rows, model_width),
        "seq",
        split_axis=2,
        concat_axis=1,
        tiled=True,
    )
    split_heads = kept_state["split_heads"]
    head_shape = split_heads[0].shape
    grad_q, grad_k, grad_v = lax.map(
        attend_backward,
        split_heads + (key_mask, kept_state["log_total"], grad_heads.reshape(head_shape)),
    )
    layout = grad_heads.shape
    back_parts = (
        lax.all_to_all(
            as_sent(grad_q.reshape(layout)), "seq", split_axis=1, concat_axis=2, tiled=True
        ),
        lax.all_to_all(
            as_sent(grad_k.reshape(layout)), "seq", split_axis=1, concat_axis=2, tiled=True
        ),
        lax.all_to_all(
            as_sent(grad_v.reshape(layout)), "seq", split_axis=1, concat_axis=2, tiled=True
        ),
    )
    grad_mixed = jnp.concatenate(
        (
            back_parts[0].reshape(-1, model_width),
            back_parts[1].reshape(-1, model_width),
            back_parts[2].reshape(-1, model_width),
        ),
        axis=1,
    )
    qkv_weight_grad = jnp.einsum(
        "ri,ro->io", kept_state["normed_low"], grad_mixed, preferred_element_type=jnp.float32
    )
    query_bias_grad = jnp.sum(back_parts[0].astype(jnp.float32), axis=(0, 1))
    value_bias_grad = jnp.sum(back_parts[2].astype(jnp.float32), axis=(0, 1))
    grad_normed = jnp.einsum("ro,io->ri", grad_mixed, qkv_full, preferred_element_type=jnp.float32)
    grad_rows_norm, norm1_gain_grad, norm1_bias_grad = kept_state["norm_one_back"](grad_normed)
    input_grad = (grad_hidden + grad_rows_norm).reshape(pair_count, part_rows, model_width)
    shard_terms = (
        lax.psum_scatter(norm1_gain_grad, "fsdp", scatter_dimension=0, tiled=True),
        lax.psum_scatter(norm1_bias_grad, "fsdp", scatter_dimension=0, tiled=True),
        lax.psum_scatter(qkv_weight_grad, "fsdp", scatter_dimension=0, tiled=True),
        lax.psum_scatter(query_bias_grad, "fsdp", scatter_dimension=0, tiled=True),
        lax.psum_scatter(value_bias_grad, "fsdp", scatter_dimension=0, tiled=True),
        lax.psum_scatter(proj_weight_grad, "fsdp", scatter_dimension=0, tiled=True),
        lax.psum_scatter(proj_bias_grad, "fsdp", scatter_dimension=0, tiled=True),
        lax.psum_scatter(norm2_gain_grad, "fsdp", scatter_dimension=0, tiled=True),
        lax.psum_scatter(norm2_bias_grad, "fsdp", scatter_dimension=0, tiled=True),
        lax.psum_scatter(up_weight_grad, "fsdp", scatter_dimension=0, tiled=True),
        lax.psum_scatter(up_bias_grad, "fsdp", scatter_dimension=0, tiled=True),
        lax.psum_scatter(down_weight_grad, "fsdp", scatter_dimension=1, tiled=True),
        lax.psum_scatter(down_bias_grad, "fsdp", scatter_dimension=0, tiled=True),
    )
    summed = lax.psum(
        (
            shard_terms[0],
            shard_terms[1],
            shard_terms[2],
            shard_terms[3],
            shard_terms[4],
            shard_terms[5],
            shard_terms[6],
            shard_terms[7],
            shard_terms[8],
            shard_terms[9],
            shard_terms[10],
            shard_terms[11],
            shard_terms[12],
        ),
        "seq",
    )
    return (
        first["output"],
        input_grad,
        summed[0],
        summed[1],
        summed[2],
        summed[3],
        summed[4],
        summed[5],
        summed[6],
        summed[7],
        summed[8],
        summed[9],
        summed[10],
        summed[11],
        summed[12],
    )


def solution(mesh):
    in_specs = (
        P("fsdp", "seq", None),
        P("fsdp", None),
        P("fsdp"),
        P("fsdp"),
        P("fsdp"),
        P("fsdp", None),
        P("fsdp"),
        P("fsdp"),
        P("fsdp", None),
        P("fsdp"),
        P("fsdp"),
        P("fsdp"),
        P("fsdp", None),
        P("fsdp"),
        P(None, "fsdp"),
        P("fsdp"),
        P("fsdp", "seq", None),
    )
    out_specs = (
        P("fsdp", "seq", None),
        P("fsdp", "seq", None),
        P("fsdp"),
        P("fsdp"),
        P("fsdp", None),
        P("fsdp"),
        P("fsdp"),
        P("fsdp", None),
        P("fsdp"),
        P("fsdp"),
        P("fsdp"),
        P("fsdp", None),
        P("fsdp"),
        P(None, "fsdp"),
        P("fsdp"),
    )
    return jax.shard_map(shards, mesh=mesh, in_specs=in_specs, out_specs=out_specs, check_vma=False)
```

profile of v0, /device:TPU:0, one launch (start us, length us, event | category | flops | bytes accessed | tf_op | source)
XLA Modules:
  0.0 1495.3 jit_solution(833111917682874269)
XLA Ops:
  14.1 19.2 %all-reduce.21 = (bf16[1152]{0:T(1024)(128)(2,1)S(1)}, bf16[1152]{0:T(1024)(128)(2,1)S(1)}, bf16[1152]{0:T(1024)(128)(2,1)S(1)}, bf16[1152]{0:T(1024)(128)(2,1)S...) all-reduce(bf16[1152]{0:T(1024)(128)(2,1)S(1)} %dynamic-update-slic, ...), channel_id=1, replica_groups=mesh['seq'=8,'fsdp'=4] {'fsdp'}, use_global_device_ids=true, to_apply=%add.1 | all-reduce | flops 13520 | bytes 54080
  35.9 61.2 %all-gather.5.cloned.1.call-done = bf16[1152,3456]{1,0:T(8,128)(2,1)} async-done(((bf16[288,3456]{1,0:T(8,128)(2,1)}), bf16[1152,3456]{1,0:T(8,128)(2,1)}) %all-gather.5.cloned.1.call-update) | async-done | bytes 7962640 | tf_op jit(solution)/shard_map/all_gather | solution.py:197
  97.1 6.0 fusion.150
  117.2 26.7 %all-to-all-done = bf16[2,184,1152]{1,0,2:T(2,128)(2,1)S(1)} async-done(((bf16[2,184,1152]{1,0,2:T(2,128)(2,1)}), bf16[2,184,1152]{1,0,2:T(2,128)(2,1)S(1)}, u32[]{:S(2)}, u32[]{:S(2)}) %all-to-all-start) | async-done | bytes 847904 | tf_op jit(solution)/shard_map/all_to_all | solution.py:125
  154.6 22.2 %all-to-all-done.1 = bf16[2,184,1152]{1,0,2:T(2,128)(2,1)S(1)} async-done(((bf16[2,184,1152]{1,0,2:T(2,128)(2,1)}), bf16[2,184,1152]{1,0,2:T(2,128)(2,1)S(1)}, u32[]{:S(2)}, u32[]{:S(2)}) %all-to-all-start.1) | async-done | bytes 847904 | tf_op jit(solution)/shard_map/all_to_all | solution.py:123
  191.9 18.5 %all-to-all-done.2 = bf16[2,184,1152]{1,0,2:T(2,128)(2,1)} async-done(((bf16[2,184,1152]{1,0,2:T(2,128)(2,1)}), bf16[2,184,1152]{1,0,2:T(2,128)(2,1)}, u32[]{:S(2)}, u32[]{:S(2)}) %all-to-all-start.2) | async-done | bytes 847904 | tf_op jit(solution)/shard_map/all_to_all | solution.py:124
  219.7 29.2 %while.42 = (s32[]{:T(128)}, bf16[4,736,2,72]{1,3,2,0:T(8,128)(2,1)}, bf16[4,736,2,72]{1,3,2,0:T(8,128)(2,1)}, bf16[4,736,2,72]{1,3,2,0:T(8,128)(2,1)S(1)}, bf16...) while((s32[]{:T(128)}, bf16[4,736,2,72]{1,3,2,0:T(8,128)(2,1)}, ...), condition=%wide.region_5.6_spmd, body=%wide.region_2.5_spmd.sunk | while | flops 318626176 | bytes 9764185 | solution.py:134
  255.4 6.0 copy.179
  267.1 19.5 %while.43 = (s32[]{:T(128)}, bf16[4,736,2,72]{1,3,2,0:T(8,128)(2,1)}, f32[4,2,736,1]{2,1,3,0:T(2,128)S(1)}, bf16[4,736,2,72]{1,3,2,0:T(8,128)(2,1)}, bf16[4,736,...) while((s32[]{:T(128)}, ...), condition=%wide.region_11.12_spmd, body=%wide.region_8.11_spmd.sunk | while | flops 325124320 | bytes 13951333 | solution.py:134
  307.1 6.1 copy.180
  317.1 26.0 %all-to-all-done.4 = bf16[2,1472,144]{2,0,1:T(2,128)(2,1)} async-done(((bf16[2,1472,144]{2,0,1:T(2,128)(2,1)}), bf16[2,1472,144]{2,0,1:T(2,128)(2,1)}, u32[]{:S(2)}, u32[]{:S(2)}) %all-to-all-start.4) | async-done | bytes 847904 | tf_op jit(solution)/shard_map/all_to_all | solution.py:137
  343.2 6.1 copy.186
  362.3 17.5 %fusion.111 = f32[368,1152]{1,0:T(8,128)} fusion(f32[368,1152]{1,0:T(8,128)} %copy-done.22, bf16[4304,1152]{0,1:T(8,128)(2,1)} %all-gather.11.cloned.1.call-done, bf16[1152,4304]{1,0:T(8,128)(2,1)} %all-gather.9.cloned.1.call-done, f32[4304]{0:T(1024)S(1)} %convert_element_type.223, f32[1152]{0:T(1024)S(1)} %convert_element_type.225, ...), kind=kOutput, calls=%fused_computation.119 | convolution fusion | flops 7317288448 | bytes 23258304 | tf_op jit(solution)/shard_map/dot_general | solution.py:157
  383.6 8.3 convolution_add_fusion
  392.0 9.9 convert_reduce_fusion
  401.9 9.9 multiply_reduce_fusion.4
  431.7 23.5 %all-to-all-done.5 = bf16[2,184,1152]{1,0,2:T(2,128)(2,1)} async-done(((bf16[2,184,1152]{1,0,2:T(2,128)(2,1)}), bf16[2,184,1152]{1,0,2:T(2,128)(2,1)}, u32[]{:S(2)}, u32[]{:S(2)}) %all-to-all-start.5) | async-done | bytes 847904 | tf_op jit(solution)/shard_map/all_to_all | solution.py:244
  467.2 37.2 %while.44 = (s32[]{:T(128)}, bf16[4,736,2,72]{1,3,2,0:T(8,128)(2,1)}, bf16[4,736,2,72]{1,3,2,0:T(8,128)(2,1)}, bf16[4,736,2,72]{1,3,2,0:T(8,128)(2,1)}, bf16[4,7...) while((s32[]{:T(128)}, ...), condition=%wide.region_18.19_spmd, body=%wide.region_16.18_spmd.sunk | while | flops 796823808 | bytes 38734360 | solution.py:253
  527.0 24.1 %all-to-all-done.6 = bf16[2,1472,144]{2,0,1:T(2,128)(2,1)S(1)} async-done(((bf16[2,1472,144]{2,0,1:T(2,128)(2,1)}), bf16[2,1472,144]{2,0,1:T(2,128)(2,1)S(1)}, u32[]{:S(2)}, u32[]{:S(2)}) %all-to-all-start.6) | async-done | bytes 847904 | tf_op jit(solution)/shard_map/all_to_all | solution.py:259
  561.7 6.0 copy.202
  567.7 24.2 %all-to-all-done.7 = bf16[2,1472,144]{2,0,1:T(2,128)(2,1)} async-done(((bf16[2,1472,144]{2,0,1:T(2,128)(2,1)}), bf16[2,1472,144]{2,0,1:T(2,128)(2,1)}, u32[]{:S(2)}, u32[]{:S(2)}) %all-to-all-start.7) | async-done | bytes 847904 | tf_op jit(solution)/shard_map/all_to_all | solution.py:262
  614.3 18.2 %all-to-all-done.8 = bf16[2,1472,144]{2,0,1:T(2,128)(2,1)} async-done(((bf16[2,1472,144]{2,0,1:T(2,128)(2,1)}), bf16[2,1472,144]{2,0,1:T(2,128)(2,1)}, u32[]{:S(2)}, u32[]{:S(2)}) %all-to-all-start.8) | async-done | bytes 847904 | tf_op jit(solution)/shard_map/all_to_all | solution.py:265
  646.8 7.9 fusion.151
  656.2 11.5 fusion.133
  668.8 13.5 fusion.104
  682.4 117.7 %reduce-scatter.5.cloned.1.call-done = f32[288,3456]{1,0:T(8,128)} async-done(((f32[1152,3456]{1,0:T(8,128)}), f32[288,3456]{1,0:T(8,128)}) %reduce-scatter.5.cloned.1.call-update) | async-done | bytes 3981328 | tf_op jit(solution)/shard_map/reduce_scatter | solution.py:288
  800.2 183.5 %reduce-scatter.9.cloned.1.call-done = f32[288,4304]{1,0:T(8,128)} async-done(((f32[1152,4304]{1,0:T(8,128)}), f32[288,4304]{1,0:T(8,128)}) %reduce-scatter.9.cloned.1.call-update) | async-done | bytes 4958224 | tf_op jit(solution)/shard_map/reduce_scatter | solution.py:295
  983.6 183.5 %reduce-scatter.11.cloned.1.call-done = f32[4304,288]{0,1:T(8,128)} async-done(((f32[4304,1152]{0,1:T(8,128)}), f32[4304,288]{0,1:T(8,128)}) %reduce-scatter.11.cloned.1.call-update) | async-done | bytes 4958224 | tf_op jit(solution)/shard_map/reduce_scatter | solution.py:297
  1174.8 10.6 fusion.134
  1185.4 17.2 %all-reduce.20 = (f32[1152]{0:T(1024)S(1)}, f32[1152]{0:T(1024)S(1)}, f32[1152]{0:T(1024)S(1)}, f32[1152]{0:T(1024)S(1)}, f32[1152]{0:T(1024)S(1)}, /*index=5*/f...) all-reduce(f32[1152]{0:T(1024)S(1)} %get-tuple-element.412, ...), channel_id=2, replica_groups=mesh['seq'=8,'fsdp'=4] {'fsdp'}, use_global_device_ids=true, to_apply=%region_22.23.clone | all-reduce | flops 13520 | bytes 108160
  1208.4 28.3 %all-reduce.18 = (f32[288]{0:T(512)}, f32[288]{0:T(512)}, f32[288]{0:T(512)}, f32[288]{0:T(512)}, f32[288]{0:T(512)}, /*index=5*/f32[288]{0:T(512)}, f32[288]{0:T(512)}, f32[1076]{0:T(1024)}, f32[288]{0:T(512)}) all-reduce(f32[288]{0:T(512)S(1)} %dynamic-slice.10, ...), channel_id=1, replica_groups=mesh['seq'=8,'fsdp'=4] {'seq'}, use_global_device_ids=true, to_apply=%region_23.24 | all-reduce | flops 3380 | bytes 27040 | tf_op jit(solution)/shard_map/psum | solution.py:300
  1239.8 237.1 %all-reduce.24.cloned.1.call-done = (f32[288,3456]{1,0:T(8,128)}, f32[288,1152]{1,0:T(8,128)}, f32[288,4304]{1,0:T(8,128)}, f32[4304,288]{0,1:T(8,128)}) async-done(((f32[288,3456]{1,0:T(8,128)}, f32[288,1152]{1,0:T(8,128)}, f32[288,4304]{1,0:T(8,128)}, f32[4304,288]{0,1:T(8,128)}), (f32[288,3456]{1,0:T(8,128)}, f32[288,1152]{1,0:T(8,128)}, f32[288,4304]{1,0:T(8,128)}, ...) | async-done | bytes 15224848 | tf_op jit(solution)/shard_map/psum | solution.py:300
  (352 shorter events, 326.8 us)
Async XLA Ops:
  7.3 89.8 %all-gather.5.cloned.1.call-start = ((), (), s32[]{:S(2)}) async-start(), calls=%async_computation.13 | async-start | bytes 9953280 | tf_op jit(solution)/shard_map/all_gather | solution.py:197
  8.0 345.4 %all-gather.7.cloned.1.call-start = ((), (), s32[]{:S(2)}) async-start(), calls=%async_computation.14 | async-start | bytes 3317760 | tf_op jit(solution)/shard_map/all_gather | solution.py:200
  8.8 353.5 %all-gather.11.cloned.1.call-start = ((), (), s32[]{:S(2)}) async-start(), calls=%async_computation.16 | async-start | bytes 12533760 | tf_op jit(solution)/shard_map/all_gather | solution.py:206
  11.7 91.4 %copy-start.34 = (f32[368]{0:T(512)}, f32[368]{0:T(512)S(1)}, u32[]{:S(2)}) copy-start(f32[368]{0:T(512)S(1)} %div.83) | copy-start | bytes 4420
  33.3 69.9 %copy-start.25 = (f32[1152]{0:T(1024)}, f32[1152]{0:T(1024)S(1)}, u32[]{:S(2)}) copy-start(f32[1152]{0:T(1024)S(1)} %convert_element_type.212) | copy-start | bytes 13828
  35.9 67.2 %copy-start.14 = (bf16[368,1152]{1,0:T(8,128)(2,1)}, bf16[368,1152]{1,0:T(8,128)(2,1)S(1)}, u32[]{:S(2)}) copy-start(bf16[368,1152]{1,0:T(8,128)(2,1)S(1)} %get-tuple-element.505) | copy-start | bytes 2543620
  110.0 33.9 %all-to-all-start = ((bf16[2,184,1152]{1,0,2:T(2,128)(2,1)}), bf16[2,184,1152]{1,0,2:T(2,128)(2,1)S(1)}, u32[]{:S(2)}, u32[]{:S(2)}) async-start(bf16[2,184,1152]{1,0,2:T(2,128)(2,1)} %copy.166), calls=%async_computation | async-start | bytes 2359296 | tf_op jit(solution)/shard_map/all_to_all | solution.py:125
  143.9 32.9 %all-to-all-start.1 = ((bf16[2,184,1152]{1,0,2:T(2,128)(2,1)}), bf16[2,184,1152]{1,0,2:T(2,128)(2,1)S(1)}, u32[]{:S(2)}, u32[]{:S(2)}) async-start(bf16[2,184,1152]{1,0,2:T(2,128)(2,1)} %copy.169), calls=%async_computation.1 | async-start | bytes 2359296 | tf_op jit(solution)/shard_map/all_to_all | solution.py:123
  176.8 33.6 %all-to-all-start.2 = ((bf16[2,184,1152]{1,0,2:T(2,128)(2,1)}), bf16[2,184,1152]{1,0,2:T(2,128)(2,1)}, u32[]{:S(2)}, u32[]{:S(2)}) async-start(bf16[2,184,1152]{1,0,2:T(2,128)(2,1)} %copy.172), calls=%async_computation.2 | async-start | bytes 2359296 | tf_op jit(solution)/shard_map/all_to_all | solution.py:124
  181.1 181.2 %all-gather.9.cloned.1.call-start = ((), (), s32[]{:S(2)}) async-start(), calls=%async_computation.15 | async-start | bytes 12533760 | tf_op jit(solution)/shard_map/all_gather | solution.py:204
  261.3 41.1 %all-to-all-start.3 = ((bf16[2,1472,144]{2,0,1:T(2,128)(2,1)}), bf16[2,1472,144]{2,0,1:T(2,128)(2,1)}, u32[]{:S(2)}, u32[]{:S(2)}) async-start(bf16[2,1472,144]{2,0,1:T(2,128)(2,1)} %copy.179), calls=%async_computation.3 | async-start | bytes 3014656 | tf_op jit(solution)/shard_map/all_to_all | solution.py:139
  292.9 13.9 copy-start.52
  302.5 40.7 %all-to-all-start.4 = ((bf16[2,1472,144]{2,0,1:T(2,128)(2,1)}), bf16[2,1472,144]{2,0,1:T(2,128)(2,1)}, u32[]{:S(2)}, u32[]{:S(2)}) async-start(bf16[2,1472,144]{2,0,1:T(2,128)(2,1)} %copy.185), calls=%async_computation.4 | async-start | bytes 3014656 | tf_op jit(solution)/shard_map/all_to_all | solution.py:137
  392.0 9.9 copy-start.7
  401.9 9.9 copy-start.31
  421.5 33.6 %all-to-all-start.5 = ((bf16[2,184,1152]{1,0,2:T(2,128)(2,1)}), bf16[2,184,1152]{1,0,2:T(2,128)(2,1)}, u32[]{:S(2)}, u32[]{:S(2)}) async-start(bf16[2,184,1152]{1,0,2:T(2,128)(2,1)} %copy.187), calls=%async_computation.5 | async-start | bytes 2359296 | tf_op jit(solution)/shard_map/all_to_all | solution.py:244
  425.8 256.6 %reduce-scatter.7.cloned.1.call-start = ((), (), s32[]{:S(2)}) async-start(), calls=%async_computation.18 | async-start | bytes 6635520 | tf_op jit(solution)/shard_map/reduce_scatter | solution.py:291
  511.1 40.1 %all-to-all-start.6 = ((bf16[2,1472,144]{2,0,1:T(2,128)(2,1)}), bf16[2,1472,144]{2,0,1:T(2,128)(2,1)S(1)}, u32[]{:S(2)}, u32[]{:S(2)}) async-start(bf16[2,1472,144]{2,0,1:T(2,128)(2,1)} %copy.195), calls=%async_computation.6 | async-start | bytes 3014656 | tf_op jit(solution)/shard_map/all_to_all | solution.py:259
  551.1 10.6 copy-start.10
  551.1 40.7 %all-to-all-start.7 = ((bf16[2,1472,144]{2,0,1:T(2,128)(2,1)}), bf16[2,1472,144]{2,0,1:T(2,128)(2,1)}, u32[]{:S(2)}, u32[]{:S(2)}) async-start(bf16[2,1472,144]{2,0,1:T(2,128)(2,1)} %copy.198), calls=%async_computation.7 | async-start | bytes 3014656 | tf_op jit(solution)/shard_map/all_to_all | solution.py:262
  591.8 40.7 %all-to-all-start.8 = ((bf16[2,1472,144]{2,0,1:T(2,128)(2,1)}), bf16[2,1472,144]{2,0,1:T(2,128)(2,1)}, u32[]{:S(2)}, u32[]{:S(2)}) async-start(bf16[2,1472,144]{2,0,1:T(2,128)(2,1)} %copy.202), calls=%async_computation.8 | async-start | bytes 3014656 | tf_op jit(solution)/shard_map/all_to_all | solution.py:265
  596.1 204.0 %reduce-scatter.5.cloned.1.call-start = ((), (), s32[]{:S(2)}) async-start(), calls=%async_computation.17 | async-start | bytes 19906560 | tf_op jit(solution)/shard_map/reduce_scatter | solution.py:288
  601.1 9.3 copy-start.8
  654.8 328.9 %reduce-scatter.9.cloned.1.call-start = ((), (), s32[]{:S(2)}) async-start(), calls=%async_computation.19 | async-start | bytes 25067520 | tf_op jit(solution)/shard_map/reduce_scatter | solution.py:295
  667.7 499.4 %reduce-scatter.11.cloned.1.call-start = ((), (), s32[]{:S(2)}) async-start(), calls=%async_computation.20 | async-start | bytes 25067520 | tf_op jit(solution)/shard_map/reduce_scatter | solution.py:297
  682.4 794.5 %all-reduce.24.cloned.1.call-start = ((), (), s32[]{:S(2)}) async-start(), calls=%async_computation.21 | async-start | bytes 30670848 | tf_op jit(solution)/shard_map/psum | solution.py:300
  1174.7 10.6 copy-start.27
  1174.7 10.6 copy-start.38
  1174.8 10.6 copy-start.39
  1174.8 28.5 %copy-start.33 = (f32[368]{0:T(512)S(1)}, f32[368]{0:T(512)}, u32[]{:S(2)}) copy-start(f32[368]{0:T(512)} %copy-done.32) | copy-start | bytes 4420
  1203.3 33.5 %copy-start.4 = (f32[368,1152]{1,0:T(8,128)S(1)}, f32[368,1152]{1,0:T(8,128)}, u32[]{:S(2)}) copy-start(f32[368,1152]{1,0:T(8,128)} %copy-done.3) | copy-start | bytes 5087236
  1203.3 33.5 %copy-start.29 = (f32[368]{0:T(512)S(1)}, f32[368]{0:T(512)}, u32[]{:S(2)}) copy-start(f32[368]{0:T(512)} %copy-done.28) | copy-start | bytes 4420
  (47 other events, 206.1 us)
Sparse Core Ops, SparseCore 0:
  10.0 87.0 all-gather.4
  98.9 39.7 all-gather.6
  140.6 101.0 all-gather.10
  243.4 101.1 all-gather.8
  431.8 62.1 reduce-scatter.6
  654.9 145.2 reduce-scatter.4
  803.3 180.2 reduce-scatter.8
  986.8 180.2 reduce-scatter.10
  1169.8 307.0 all-reduce.23
where the time goes:
time: 1500 us
  waiting for transfers between devices  973 us (65%)
  local copies, waits for them, and re-layouts  185 us (12%)
  matrix products  183 us (12%)
  blocking collectives  64.7 us (4%)
  starting transfers between devices  39.2 us (3%)
  other arithmetic  32.1 us (2%)
  between operations  17.8 us (1%)
    psum x1, waiting for transfers between devices, shards(): lax.psum((shard_terms[0], shard_terms[1], shard_terms[2], shard_terms[3],...  237 us
    reduce_scatter x1, waiting for transfers between devices, shards(): lax.psum_scatter(down_weight_grad, 'fsdp', scatter_dimension=1, tiled=True)  183 us
    reduce_scatter x1, waiting for transfers between devices, shards(): lax.psum_scatter(up_weight_grad, 'fsdp', scatter_dimension=0, tiled=True)  183 us
    reduce_scatter x1, waiting for transfers between devices, shards(): lax.psum_scatter(qkv_weight_grad, 'fsdp', scatter_dimension=0, tiled=True)  118 us
    all_gather x1, waiting for transfers between devices, shards(): lax.all_gather(qkv_weight, 'fsdp', axis=0, tiled=True)  61.2 us
    unnamed x2, blocking collectives  36.4 us
  transfers between devices with their start and end apart: 18, of which 14 were waited for; matrix products, arithmetic and copies ran while one was open for 21% of the time, Pallas kernels for 0%

commit v1 on v0

v1 whole, which is shorter than its diff:
```python
import jax
import jax.numpy as jnp
from jax import lax
from jax.sharding import Mesh
from jax.sharding import PartitionSpec as P

HEADS = 16
HEAD = 72
epsilon = 1e-06

SEQ = ("zh", "zl", "core")
ZAX = ("zh", "zl")
GROUP = ("zl", "core")


def layer_norm(values, gain_vec, bias_vec):
    row_mean = jnp.mean(values, axis=-1, keepdims=True)
    centered = values - row_mean
    variance = jnp.mean(centered * centered, axis=-1, keepdims=True)
    return centered * lax.rsqrt(variance + epsilon) * gain_vec + bias_vec


def gelu_tanh(values):
    return (
        0.5
        * values
        * (1.0 + jnp.tanh(0.7978845608028654 * (values + 0.044715 * values * values * values)))
    )


def gather_weight(w, axis):
    half = w.shape[axis] // 2
    core = lax.axis_index("core")
    piece = lax.dynamic_slice_in_dim(w, core * half, half, axis=axis)
    return lax.all_gather(piece, ("fsdp", "core"), axis=axis, tiled=True)


def reduce_weight(g, axis):
    part = lax.psum_scatter(
        g.astype(jnp.bfloat16), ("fsdp", "core"), scatter_dimension=axis, tiled=True
    )
    part = lax.psum(part.astype(jnp.float32), ZAX)
    return lax.all_gather(part, "core", axis=axis, tiled=True)


def shards(
    block_input,
    key_mask,
    slot_flags,
    norm1_gain,
    norm1_bias,
    qkv_weight,
    query_bias,
    value_bias,
    proj_weight,
    proj_bias,
    norm2_gain,
    norm2_bias,
    up_weight,
    up_bias,
    down_weight,
    down_bias,
    out_grad,
):
    f32, bf16 = jnp.float32, jnp.bfloat16
    pairs, part_rows, width = block_input.shape
    group = lax.axis_size("zl") * lax.axis_size("core")
    local_heads = HEADS // group
    slot_len = part_rows * group
    zh = lax.axis_index("zh")
    scale = HEAD ** (-0.5)

    vectors = (norm1_gain, norm1_bias, query_bias, value_bias, proj_bias, norm2_gain,
               norm2_bias, up_bias, down_bias)
    sizes = [v.shape[0] for v in vectors]
    packed = jnp.concatenate([v.astype(f32) for v in vectors])
    packed = lax.all_gather(packed, "fsdp", axis=0, tiled=False)
    full_vectors = []
    at = 0
    for n in sizes:
        full_vectors.append(packed[:, at : at + n].reshape(-1))
        at += n
    g1, b1, bq, bv, bproj, g2, b2, bup, bdown = full_vectors

    w_qkv = gather_weight(qkv_weight, 0)
    w_proj = gather_weight(proj_weight, 0)
    w_up = gather_weight(up_weight, 0)
    w_down = gather_weight(down_weight, 1)

    flags = slot_flags.astype(f32).reshape(pairs, 2)
    row_flags = lax.dynamic_index_in_dim(flags, zh, axis=1, keepdims=False)
    live = lax.dynamic_index_in_dim(key_mask.reshape(pairs, 2, -1), zh, axis=1, keepdims=False)
    mask_bias = (live.astype(f32) - 1.0) * 10000.0

    rows = block_input.reshape(pairs * part_rows, width).astype(f32)
    normed, norm_one_back = jax.vjp(layer_norm, rows, g1, b1)
    normed_low = normed.astype(bf16)
    mixed = jnp.dot(normed_low, w_qkv, preferred_element_type=f32)
    q = (mixed[:, :width] + bq).astype(bf16)
    k = mixed[:, width : 2 * width].astype(bf16)
    v = (mixed[:, 2 * width :] + bv).astype(bf16)
    qkv_tok = jnp.stack([q, k, v]).reshape(3, pairs, part_rows, width)
    qkv_heads = lax.all_to_all(qkv_tok, GROUP, split_axis=3, concat_axis=2, tiled=True)
    qkv_heads = qkv_heads.reshape(3, pairs, slot_len, local_heads, HEAD)
    qh, kh, vh = qkv_heads[0], qkv_heads[1], qkv_heads[2]

    scores = jnp.einsum("pqhd,pkhd->phqk", qh, kh, preferred_element_type=f32) * scale
    shifted = scores + mask_bias[:, None, None, :]
    row_max = jnp.max(shifted, axis=-1, keepdims=True)
    exp_terms = jnp.exp(shifted - row_max)
    probs = exp_terms / jnp.sum(exp_terms, axis=-1, keepdims=True)
    weights_low = probs.astype(bf16)
    attended = jnp.einsum("phqk,pkhd->pqhd", weights_low, vh, preferred_element_type=f32)
    attended = attended.astype(bf16).reshape(pairs, slot_len, local_heads * HEAD)
    merged = lax.all_to_all(attended, GROUP, split_axis=1, concat_axis=2, tiled=True)
    merged_rows = merged.reshape(pairs * part_rows, width)

    hidden = rows + jnp.dot(merged_rows, w_proj, preferred_element_type=f32) + bproj
    second, norm_two_back = jax.vjp(layer_norm, hidden, g2, b2)
    second_low = second.astype(bf16)
    gate_in = jnp.dot(second_low, w_up, preferred_element_type=f32) + bup
    active, gelu_back = jax.vjp(gelu_tanh, gate_in)
    active_low = active.astype(bf16)
    result = hidden + jnp.dot(active_low, w_down, preferred_element_type=f32) + bdown
    row_flag_rows = jnp.repeat(row_flags, part_rows)[:, None]
    output = (result * row_flag_rows).astype(bf16).reshape(pairs, part_rows, width)

    grad_rows = out_grad.reshape(pairs * part_rows, width).astype(f32) * row_flag_rows
    grad_low = grad_rows.astype(bf16)
    down_weight_grad = jnp.dot(active_low.T, grad_low, preferred_element_type=f32)
    down_bias_grad = jnp.sum(grad_rows, axis=0)
    grad_active = jnp.dot(grad_low, w_down.T, preferred_element_type=f32)
    grad_gate = gelu_back(grad_active)[0].astype(bf16)
    up_weight_grad = jnp.dot(second_low.T, grad_gate, preferred_element_type=f32)
    up_bias_grad = jnp.sum(grad_gate.astype(f32), axis=0)
    grad_second = jnp.dot(grad_gate, w_up.T, preferred_element_type=f32)
    grad_hidden_norm, norm2_gain_grad, norm2_bias_grad = norm_two_back(grad_second)
    grad_hidden = grad_rows + grad_hidden_norm
    grad_branch = grad_hidden.astype(bf16)
    proj_weight_grad = jnp.dot(merged_rows.T, grad_branch, preferred_element_type=f32)
    proj_bias_grad = jnp.sum(grad_branch.astype(f32), axis=0)
    grad_merged = jnp.dot(grad_branch, w_proj.T, preferred_element_type=f32).astype(bf16)
    grad_heads = lax.all_to_all(
        grad_merged.reshape(pairs, part_rows, width), GROUP, split_axis=2, concat_axis=1, tiled=True
    ).reshape(pairs, slot_len, local_heads, HEAD)

    grad_probs = jnp.einsum("pqhd,pkhd->phqk", grad_heads, vh, preferred_element_type=f32)
    row_dot = jnp.sum(probs * grad_probs, axis=-1, keepdims=True)
    grad_scores = (probs * (grad_probs - row_dot)).astype(bf16)
    dq = (jnp.einsum("phqk,pkhd->pqhd", grad_scores, kh, preferred_element_type=f32) * scale).astype(bf16)
    dk = (jnp.einsum("phqk,pqhd->pkhd", grad_scores, qh, preferred_element_type=f32) * scale).astype(bf16)
    dv = jnp.einsum("phqk,pqhd->pkhd", weights_low, grad_heads, preferred_element_type=f32).astype(bf16)
    dqkv = jnp.stack([dq, dk, dv]).reshape(3, pairs, slot_len, local_heads * HEAD)
    dqkv_tok = lax.all_to_all(dqkv, GROUP, split_axis=2, concat_axis=3, tiled=True)
    dqkv_tok = dqkv_tok.reshape(3, pairs * part_rows, width)
    grad_mixed = jnp.concatenate([dqkv_tok[0], dqkv_tok[1], dqkv_tok[2]], axis=1)
    qkv_weight_grad = jnp.dot(normed_low.T, grad_mixed, preferred_element_type=f32)
    query_bias_grad = jnp.sum(dqkv_tok[0].astype(f32), axis=0)
    value_bias_grad = jnp.sum(dqkv_tok[2].astype(f32), axis=0)
    grad_normed = jnp.dot(grad_mixed, w_qkv.T, preferred_element_type=f32)
    grad_rows_norm, norm1_gain_grad, norm1_bias_grad = norm_one_back(grad_normed)
    input_grad = (grad_hidden + grad_rows_norm).reshape(pairs, part_rows, width)

    vec_grads = (norm1_gain_grad, norm1_bias_grad, query_bias_grad, value_bias_grad,
                 proj_bias_grad, norm2_gain_grad, norm2_bias_grad, up_bias_grad, down_bias_grad)
    fsdp = lax.axis_size("fsdp")
    stacked = jnp.concatenate([g.reshape(fsdp, -1) for g in vec_grads], axis=1)
    stacked = lax.psum_scatter(stacked, "fsdp", scatter_dimension=0, tiled=True)
    stacked = lax.psum(stacked, SEQ).reshape(-1)
    vec_out = []
    at = 0
    for g in vec_grads:
        n = g.shape[0] // fsdp
        vec_out.append(stacked[at : at + n])
        at += n
    (n1g, n1b, qb, vb, pb, n2g, n2b, ub, db) = vec_out

    qkv_g = reduce_weight(qkv_weight_grad, 0)
    proj_g = reduce_weight(proj_weight_grad, 0)
    up_g = reduce_weight(up_weight_grad, 0)
    down_g = reduce_weight(down_weight_grad, 1)

    return (output, input_grad, n1g, n1b, qkv_g, qb, vb, proj_g, pb, n2g, n2b, up_g, ub, down_g, db)


def solution(mesh):
    seq_n = mesh.shape["seq"]
    fsdp_n = mesh.shape["fsdp"]
    devices = mesh.devices.reshape(2, seq_n // 4, 2, fsdp_n)
    inner = Mesh(devices, ("zh", "zl", "core", "fsdp"))
    tok = P("fsdp", SEQ, None)
    vec = P("fsdp")
    rows = P("fsdp", None)
    in_specs = (tok, rows, vec, vec, vec, rows, vec, vec, rows, vec, vec, vec, rows, vec,
                P(None, "fsdp"), vec, tok)
    out_specs = (tok, tok, vec, vec, rows, vec, vec, rows, vec, vec, vec, rows, vec,
                 P(None, "fsdp"), vec)
    return jax.shard_map(shards, mesh=inner, in_specs=in_specs, out_specs=out_specs, check_vma=False)
```

time: 1500 us -> 915 us (0.61)
  waiting for transfers between devices: 973 us -> 161 us
  blocking collectives: 64.7 us -> 368 us
  local copies, waits for them, and re-layouts: 185 us -> 148 us
  matrix products: 183 us -> 154 us
  starting transfers between devices: 39.2 us -> 13.9 us
    reduce_scatter x4, waiting for transfers between devices: 485 us -> 74.1 us  [reduce_weight(): lax.psum_scatter(g.astype(jnp.bfloat16), ('fsdp', 'core'), scatter_dimens...]
    psum x1 -> x2, blocking collectives: 28.3 us -> 288 us  [the longest x1 262 us: reduce_weight(): part = lax.psum(part.astype(jnp.float32), ZAX)]
    psum x1 -> x0, waiting for transfers between devices: 237 us -> none  [shards(): lax.psum((shard_terms[0], shard_terms[1], shard_terms[2], shard_terms[3],...]
    all_to_all x9 -> x3, waiting for transfers between devices: 187 us -> 58.7 us  [the longest x1 41.1 us: shards(): lax.all_to_all(qkv_tok, GROUP, split_axis=3, concat_axis=2, tiled=True)]
    reshape x24 -> x13, local copies, waits for them, and re-layouts: 90.4 us -> 12.9 us  [the longest x1 4.12 us: shards(): grad_merged.reshape(pairs, part_rows, width)]
    all_to_all x0 -> x1, blocking collectives: none -> 43.3 us  [shards(): lax.all_to_all(dqkv, GROUP, split_axis=2, concat_axis=3, tiled=True)]
    all_gather x4 -> x8, waiting for transfers between devices: 61.2 us -> 26.9 us  [the longest x4 26.9 us: gather_weight(): return lax.all_gather(piece, ('fsdp', 'core'), axis=axis, tiled=True)]
    slice x1 -> x13, local copies, waits for them, and re-layouts: 2.8 us -> 35.2 us  [the longest x4 16.2 us: shards(): qh, kh, vh = (qkv_heads[0], qkv_heads[1], qkv_heads[2])]
  transfers between devices with their start and end apart: 18 -> 15, of which waited for: 14 -> 6; matrix products, arithmetic and copies ran while one was open for 21% -> 33% of each run, Pallas kernels for 0% -> 0%
where the time goes in v1:
time: 915 us; the launch traced here: 907 us
  blocking collectives  368 us (40%)
  waiting for transfers between devices  161 us (18%)
  matrix products  154 us (17%)
  local copies, waits for them, and re-layouts  148 us (16%)
  other arithmetic  46.4 us (5%)
  between operations  15.9 us (2%)
  starting transfers between devices  13.9 us (2%)
    psum x1, blocking collectives, reduce_weight(): part = lax.psum(part.astype(jnp.float32), ZAX)  262 us
    reduce_scatter x4, waiting for transfers between devices, reduce_weight(): lax.psum_scatter(g.astype(jnp.bfloat16), ('fsdp', 'core'), scatter_dimens...  74.1 us
    all_to_all x1, blocking collectives, shards(): lax.all_to_all(dqkv, GROUP, split_axis=2, concat_axis=3, tiled=True)  43.3 us
    all_to_all x1, waiting for transfers between devices, shards(): lax.all_to_all(qkv_tok, GROUP, split_axis=3, concat_axis=2, tiled=True)  41.1 us
    unnamed x2, blocking collectives  36.9 us
    all_gather x4, waiting for transfers between devices, gather_weight(): return lax.all_gather(piece, ('fsdp', 'core'), axis=axis, tiled=True)  26.9 us
    psum x1, blocking collectives, shards(): stacked = lax.psum(stacked, SEQ).reshape(-1)  25.9 us
    unnamed x111, local copies, waits for them, and re-layouts  21.6 us
  transfers between devices with their start and end apart: 15, of which 6 were waited for; matrix products, arithmetic and copies ran while one was open for 33% of the time, Pallas kernels for 0%

profile of v1, /device:TPU:0, one launch (start us, length us, event | category | flops | bytes accessed | tf_op | source)
XLA Modules:
  0.0 907.2 jit_solution(6232372742852315515)
XLA Ops:
  17.0 20.7 %all-reduce = f32[13520]{0:T(1024)S(1)} all-reduce(f32[13520]{0:T(1024)S(1)} %convert_dynamic-update-slice_fusion), channel_id=2, replica_groups=mesh['zh'=2,'zl'=2,'core'=2,'fsdp'=4] {'fsdp'}, use_global_device_ids=true, to_apply=%add | all-reduce | flops 13520 | bytes 108160
  40.4 26.9 %all-gather.10.cloned.1.call-done = bf16[1152,3456]{1,0:T(8,128)(2,1)} async-done(((bf16[144,3456]{1,0:T(8,128)(2,1)}), bf16[1152,3456]{1,0:T(8,128)(2,1)}) %all-gather.10.cloned.1.call-update) | async-done | bytes 7962640 | tf_op jit(solution)/shard_map/all_gather | solution.py:35
  67.3 6.0 fusion.46
  87.0 8.5 pad_maximum_fusion
  95.5 5.1 all-to-all-start
  100.7 41.1 %all-to-all-done = bf16[3,2,184,1152]{2,1,0,3:T(2,128)(2,1)} async-done(((bf16[3,2,184,1152]{2,1,0,3:T(2,128)(2,1)}), bf16[3,2,184,1152]{2,1,0,3:T(2,128)(2,1)}, u32[]{:S(2)}, u32[]{:S(2)}) %all-to-all-start) | async-done | bytes 2543648 | tf_op jit(solution)/shard_map/all_to_all | solution.py:103
  141.8 12.6 %copy.92 = bf16[3,2,184,4,288]{4,3,2,1,0:T(4,128)(2,1)} copy(bf16[3,2,184,4,288]{2,1,0,4,3:T(2,128)(2,1)} %bitcast.5) | data formatting | bytes 5087232 | tf_op jit(solution)/shard_map/all_to_all | solution.py:103
  178.8 9.5 %fusion.44 = (f32[2,4,736]{2,1,0:T(4,128)S(1)}, f32[2,4,736,736]{2,3,1,0:T(8,128)}) fusion(f32[2,736]{1,0:T(2,128)S(1)} %fusion.32, bf16[2,736,4,72]{1,3,2,0:T(8,128)(2,1)S(1)} %squeeze.27, bf16[2,736,4,72]{1,3,2,0:T(8,128)(2,1)S(1)} %squeeze.28), kind=kOutput, calls=%fused_computation.113 | convolution fusion | flops 641368768 | bytes 19059456 | tf_op jit(solution)/shard_map/sub | solution.py:110
  188.3 8.1 fusion.21
  205.6 12.5 %all-to-all-done.1 = bf16[2,736,288]{2,0,1:T(2,128)(2,1)S(1)} async-done(((bf16[2,736,288]{2,0,1:T(2,128)(2,1)}), bf16[2,736,288]{2,0,1:T(2,128)(2,1)S(1)}, u32[]{:S(2)}, u32[]{:S(2)}) %all-to-all-start.1) | async-done | bytes 847904 | tf_op jit(solution)/shard_map/all_to_all | solution.py:115
  226.7 11.7 %convolution_add_fusion = f32[368,4304]{1,0:T(8,128)} fusion(bf16[1152,4304]{1,0:T(8,128)(2,1)} %all-gather.14.cloned.1.call-done, f32[4304]{0:T(1024)S(1)} %add.181, f32[368,1152]{1,0:T(8,128)} %copy-done.8, f32[1152]{0:T(1024)S(1)} %add.178, f32[1152]{0:T(1024)S(1)} %mul.237, f32[368]{0:T(512)S(1)} %fusion.33, f32[368]{0:T(512)S(1)} %broadcast_multiply_fusion), kind=kOutput, calls=%fused_computation.17 | convolution fusion | flops 3652944640 | bytes 17977024 | tf_op jit(solution)/shard_map/dot_general | solution.py:121
  238.4 12.3 %convert_reduce_fusion = (f32[4304]{0:T(1024)S(1)}, bf16[368,4304]{1,0:T(8,128)(2,1)S(1)}) fusion(f32[368,4304]{1,0:T(8,128)} %convolution_add_fusion, bf16[368,1152]{1,0:T(8,128)(2,1)} %fusion.20, bf16[4304,1152]{0,1:T(8,128)(2,1)} %all-gather.16.cloned.1.call-done), kind=kOutput, calls=%fused_computation.24 | convolution fusion | flops 3690417408 | bytes 20284736 | tf_op jit(solution)/shard_map/dot_general | solution.py:132
  250.7 9.6 %multiply_reduce_fusion.2 = (f32[1152]{0:T(1024)S(1)}, f32[368]{0:T(512)S(1)}, f32[1152]{0:T(1024)S(1)}, f32[368,1152]{1,0:T(8,128)S(1)}) fusion(f32[368,1152]{1,0:T(8,128)S(1)} %copy-done.9, f32[368]{0:T(512)S(1)} %fusion.33, f32[368]{0:T(512)S(1)} %broadcast_multiply_fusion, f32[1152]{0:T(1024)S(1)} %mul.237, ...), kind=kOutput, calls=%fused_computation.53 | convolution fusion | flops 3652630016 | bytes 16493888 | tf_op jit(solution)/shard_map/dot_general | solution.py:136
  265.5 10.4 %convolution_convert_fusion = bf16[4304,1152]{0,1:T(8,128)(2,1)} fusion(bf16[368,1152]{1,0:T(8,128)(2,1)} %fusion.20, f32[368,4304]{1,0:T(8,128)} %convolution_add_fusion), kind=kOutput, calls=%fused_computation.1 | convolution fusion | flops 3668454144 | bytes 17099776 | tf_op jit(solution)/shard_map/dot_general | solution.py:130
  288.8 10.7 %convolution_convert_fusion.1 = bf16[1152,4304]{1,0:T(8,128)(2,1)} fusion(bf16[368,4304]{1,0:T(8,128)(2,1)} %copy-done.48, f32[368,1152]{1,0:T(8,128)} %copy-done.8, f32[1152]{0:T(1024)S(1)} %add.178, f32[1152]{0:T(1024)S(1)} %mul.237, f32[368]{0:T(512)S(1)} %fusion.33, f32[368]{0:T(512)S(1)} %broadcast_multiply_fusion), kind=kOutput, calls=%fused_computation.2 | convolution fusion | flops 3656318976 | bytes 14792064 | tf_op jit(solution)/shard_map/dot_general | solution.py:134
  299.6 5.1 all-to-all-done.2
  311.1 10.7 %fusion.24 = bf16[2,4,72,736]{3,2,1,0:T(8,128)(2,1)} fusion(bf16[2,736,4,72]{1,3,2,0:T(8,128)(2,1)} %reshape.248, f32[2,4,736,736]{2,3,1,0:T(8,128)} %get-tuple-element.62, f32[2,4,736]{2,1,0:T(4,128)S(1)} %get-tuple-element.61), kind=kOutput, calls=%fused_computation.66 | convolution fusion | flops 633124864 | bytes 19053568 | tf_op jit(solution)/shard_map/phqk,pqhd->pkhd/dot_general | solution.py:152
  321.8 4.9 copy.81
  326.7 13.6 %multiply_reduce_fusion = (f32[2,4,736]{2,1,0:T(4,128)S(1)}, f32[2,4,736,736]{2,3,1,0:T(8,128)}) fusion(f32[2,4,736,736]{2,3,1,0:T(8,128)} %get-tuple-element.62, f32[2,4,736]{2,1,0:T(4,128)S(1)} %get-tuple-element.61, bf16[2,736,4,72]{1,3,2,0:T(8,128)(2,1)} %reshape.248, bf16[2,736,4,72]{1,3,2,0:T(8,128)(2,1)} %squeeze.26), kind=kOutput, calls=%fused_computation.4 | convolution fusion | flops 637028608 | bytes 36411392 | tf_op jit(solution)/shard_map/pqhd,pkhd->phqk/dot_general | solution.py:147
  340.3 13.0 %multiply_convert_fusion = bf16[2,4,736,736]{2,3,1,0:T(8,128)(2,1)S(1)} fusion(f32[2,4,736,736]{2,3,1,0:T(8,128)} %get-tuple-element.67, f32[2,4,736]{2,1,0:T(4,128)S(1)} %get-tuple-element.66, f32[2,4,736,736]{2,3,1,0:T(8,128)} %get-tuple-element.62, f32[2,4,736]{2,1,0:T(4,128)S(1)} %get-tuple-element.61), kind=kLoop, calls=%fused_computation.3 | loop fusion | flops 17334272 | bytes 43382784 | tf_op jit(solution)/shard_map/convert_element_type | solution.py:149
  361.9 6.5 multiply_convert_fusion.3
  368.4 4.7 copy.79
  373.1 7.7 pad_maximum_fusion.1
  380.8 43.3 %all_to_all.60 = bf16[3,2,736,288]{3,1,0,2:T(2,128)(2,1)} all-to-all(bf16[3,2,736,288]{3,1,0,2:T(2,128)(2,1)S(1)} %pad_maximum_fusion.1), channel_id=1, replica_groups=mesh['zh'=2,'zl'=2,'core'=2,'fsdp'=4] {'zl','core'}, dimensions={2} | all-to-all | bytes 5087232 | tf_op jit(solution)/shard_map/all_to_all | solution.py:154
  424.0 13.0 %copy.97 = bf16[3,2,4,184,288]{3,2,4,1,0:T(4,128)(2,1)} copy(bf16[3,2,4,184,288]{4,1,0,3,2:T(2,128)(2,1)} %bitcast.99) | data formatting | bytes 5087232 | tf_op jit(solution)/shard_map/all_to_all | solution.py:154
  466.4 6.6 convolution_convert_fusion.2
  474.4 72.8 %reduce-scatter.5.cloned.1.call-done = bf16[144,3456]{1,0:T(8,128)(2,1)} async-done(((bf16[1152,3456]{1,0:T(8,128)(2,1)}), bf16[144,3456]{1,0:T(8,128)(2,1)}) %reduce-scatter.5.cloned.1.call-update) | async-done | bytes 995344 | tf_op jit(solution)/shard_map/reduce_scatter | solution.py:39
  547.2 262.0 %all-reduce.4 = (f32[144,3456]{1,0:T(8,128)}, f32[144,1152]{1,0:T(8,128)}, f32[144,4304]{1,0:T(8,128)}, f32[4304,144]{0,1:T(8,128)}) all-reduce(bf16[144,3456]{1,0:T(8,128)(2,1)} %reduce-scatter.5.cloned.1.call-done, ...), channel_id=1, replica_groups=mesh['zh'=2,'zl'=2,'core'=2,'fsdp'=4] {'zh','zl'}, use_global_device_ids=true, to_apply=%region_23.24 | all-reduce | flops 1903104 | bytes 11418624 | tf_op jit(solution)/shard_map/psum | solution.py:42
  811.6 12.4 %fusion.17 = bf16[368,1152]{1,0:T(8,128)(2,1)} fusion(f32[368,1152]{1,0:T(8,128)} %copy-done.8, bf16[4304,1152]{0,1:T(8,128)(2,1)} %all-gather.16.cloned.1.call-done, f32[368]{0:T(512)S(1)} %mul.246, f32[1152]{0:T(1024)S(1)} %add.187, f32[368,4304]{1,0:T(8,128)} %convolution_add_fusion), kind=kOutput, calls=%fused_computation.37 | convolution fusion | flops 3665191680 | bytes 18801600 | tf_op jit(solution)/shard_map/dot_general | solution.py:124
  825.6 10.8 %fusion.36 = (f32[1152]{0:T(1024)S(1)}, f32[368]{0:T(512)S(1)}, f32[1152]{0:T(1024)S(1)}, f32[368,1152]{1,0:T(8,128)}) fusion(f32[368,1152]{1,0:T(8,128)} %get-tuple-element.49, f32[1152]{0:T(1024)S(1)} %copy-done.26, f32[368]{0:T(512)S(1)} %copy-done.33, f32[368]{0:T(512)S(1)} %copy-done.31, bf16[2,184,1152]{2,1,0:T(8,128)(2,1)S(1)} %copy-done.5, ...), kind=kOutput, calls=%fused_computation.107 | convolution fusion | flops 2934058496 | bytes 14763840 | tf_op jit(solution)/shard_map/dot_general | solution.py:160
  841.5 16.1 %all-reduce.1 = f32[4,3380]{1,0:T(4,128)S(1)} all-reduce(f32[4,3380]{1,0:T(4,128)S(1)} %concatenate.14), channel_id=3, replica_groups=mesh['zh'=2,'zl'=2,'core'=2,'fsdp'=4] {'fsdp'}, use_global_device_ids=true, to_apply=%region_20.21.clone | all-reduce | flops 13520 | bytes 108160
  858.3 25.9 %psum.35 = f32[1,3380]{1,0:T(1,128)S(1)} all-reduce(f32[1,3380]{1,0:T(1,128)S(1)} %constant_dynamic-slice_fusion.6), channel_id=1, replica_groups=mesh['zh'=2,'zl'=2,'core'=2,'fsdp'=4] {'zh','zl','core'}, use_global_device_ids=true, to_apply=%region_21.22 | all-reduce | flops 3380 | bytes 27040 | tf_op jit(solution)/shard_map/psum | solution.py:169
  (240 shorter events, 156.5 us)
Async XLA Ops:
  7.2 60.1 %all-gather.10.cloned.1.call-start = ((), (), s32[]{:S(2)}) async-start(), calls=%async_computation.8 | async-start | bytes 8957952 | tf_op jit(solution)/shard_map/all_gather | solution.py:35
  9.7 211.9 %all-gather.12.cloned.1.call-start = ((), (), s32[]{:S(2)}) async-start(), calls=%async_computation.9 | async-start | bytes 2985984 | tf_op jit(solution)/shard_map/all_gather | solution.py:35
  10.6 216.1 %all-gather.14.cloned.1.call-start = ((), (), s32[]{:S(2)}) async-start(), calls=%async_computation.10 | async-start | bytes 11280384 | tf_op jit(solution)/shard_map/all_gather | solution.py:35
  11.9 226.5 %all-gather.16.cloned.1.call-start = ((), (), s32[]{:S(2)}) async-start(), calls=%async_computation.11 | async-start | bytes 11280384 | tf_op jit(solution)/shard_map/all_gather | solution.py:35
  14.9 58.5 %copy-start.30 = (f32[368]{0:T(512)}, f32[368]{0:T(512)S(1)}, u32[]{:S(2)}) copy-start(f32[368]{0:T(512)S(1)} %div.47) | copy-start | bytes 4420
  15.3 58.0 %copy-start.32 = (f32[368]{0:T(512)}, f32[368]{0:T(512)S(1)}, u32[]{:S(2)}) copy-start(f32[368]{0:T(512)S(1)} %rsqrt.20) | copy-start | bytes 4420
  38.6 34.8 %copy-start.25 = (f32[1152]{0:T(1024)}, f32[1152]{0:T(1024)S(1)}, u32[]{:S(2)}) copy-start(f32[1152]{0:T(1024)S(1)} %mul.225) | copy-start | bytes 13828
  40.4 33.0 %copy-start.20 = (bf16[368,1152]{1,0:T(8,128)(2,1)}, bf16[368,1152]{1,0:T(8,128)(2,1)S(1)}, u32[]{:S(2)}) copy-start(bf16[368,1152]{1,0:T(8,128)(2,1)S(1)} %get-tuple-element.50) | copy-start | bytes 2543620
  95.5 46.2 %all-to-all-start = ((bf16[3,2,184,1152]{2,1,0,3:T(2,128)(2,1)}), bf16[3,2,184,1152]{2,1,0,3:T(2,128)(2,1)}, u32[]{:S(2)}, u32[]{:S(2)}) async-start(bf16[3,2,184,1152]{2,1,0,3:T(2,128)(2,1)} %pad_maximum_fusion), calls=%async_computation | async-start | bytes 7077888 | tf_op jit(solution)/shard_map/all_to_all | solution.py:103
  164.3 14.6 %copy-start.11 = (bf16[2,736,4,72]{1,3,2,0:T(8,128)(2,1)}, bf16[2,736,4,72]{1,3,2,0:T(8,128)(2,1)S(1)}, u32[]{:S(2)}) copy-start(bf16[2,736,4,72]{1,3,2,0:T(8,128)(2,1)S(1)} %squeeze.28) | copy-start | bytes 2543620
  171.2 17.2 %copy-start.13 = (bf16[2,736,4,72]{1,3,2,0:T(8,128)(2,1)}, bf16[2,736,4,72]{1,3,2,0:T(8,128)(2,1)S(1)}, u32[]{:S(2)}) copy-start(bf16[2,736,4,72]{1,3,2,0:T(8,128)(2,1)S(1)} %squeeze.27) | copy-start | bytes 2543620
  196.5 6.9 copy-start.47
  196.5 8.0 copy-start.6
  199.3 18.8 %all-to-all-start.1 = ((bf16[2,736,288]{2,0,1:T(2,128)(2,1)}), bf16[2,736,288]{2,0,1:T(2,128)(2,1)S(1)}, u32[]{:S(2)}, u32[]{:S(2)}) async-start(bf16[2,736,288]{2,0,1:T(2,128)(2,1)} %copy.70), calls=%async_computation.1 | async-start | bytes 2260992 | tf_op jit(solution)/shard_map/all_to_all | solution.py:115
  202.8 270.3 %reduce-scatter.7.cloned.1.call-start = ((), (), s32[]{:S(2)}) async-start(), calls=%async_computation.14 | async-start | bytes 2985984 | tf_op jit(solution)/shard_map/reduce_scatter | solution.py:39
  238.4 12.3 %copy-start.9 = (f32[368,1152]{1,0:T(8,128)S(1)}, f32[368,1152]{1,0:T(8,128)}, u32[]{:S(2)}) copy-start(f32[368,1152]{1,0:T(8,128)} %copy-done.8) | copy-start | bytes 5087236
  250.7 9.6 %copy-start.48 = (bf16[368,4304]{1,0:T(8,128)(2,1)}, bf16[368,4304]{1,0:T(8,128)(2,1)S(1)}, u32[]{:S(2)}) copy-start(bf16[368,4304]{1,0:T(8,128)(2,1)S(1)} %get-tuple-element.36) | copy-start | bytes 9503236
  250.7 9.6 %copy-start.10 = (f32[368,1152]{1,0:T(8,128)S(1)}, f32[368,1152]{1,0:T(8,128)}, u32[]{:S(2)}) copy-start(f32[368,1152]{1,0:T(8,128)} %copy-done.8) | copy-start | bytes 5087236
  265.4 207.7 %reduce-scatter.11.cloned.1.call-start = ((), (), s32[]{:S(2)}) async-start(), calls=%async_computation.18 | async-start | bytes 11280384 | tf_op jit(solution)/shard_map/reduce_scatter | solution.py:39
  284.5 20.2 %all-to-all-start.2 = ((bf16[2,184,1152]{1,0,2:T(2,128)(2,1)}), bf16[2,184,1152]{1,0,2:T(2,128)(2,1)}, u32[]{:S(2)}, u32[]{:S(2)}) async-start(bf16[2,184,1152]{1,0,2:T(2,128)(2,1)} %copy.73), calls=%async_computation.2 | async-start | bytes 2359296 | tf_op jit(solution)/shard_map/all_to_all | solution.py:143
  288.8 185.6 %reduce-scatter.9.cloned.1.call-start = ((), (), s32[]{:S(2)}) async-start(), calls=%async_computation.16 | async-start | bytes 11280384 | tf_op jit(solution)/shard_map/reduce_scatter | solution.py:39
  299.5 247.7 %reduce-scatter.5.cloned.1.call-start = ((), (), s32[]{:S(2)}) async-start(), calls=%async_computation.12 | async-start | bytes 8957952 | tf_op jit(solution)/shard_map/reduce_scatter | solution.py:39
  340.3 13.0 %copy-start.14 = (bf16[2,736,4,72]{1,3,2,0:T(8,128)(2,1)S(1)}, bf16[2,736,4,72]{1,3,2,0:T(8,128)(2,1)}, u32[]{:S(2)}) copy-start(bf16[2,736,4,72]{1,3,2,0:T(8,128)(2,1)} %copy-done.13) | copy-start | bytes 2543620
  473.0 415.6 %all-gather.20.cloned.1.call-start = ((), (), s32[]{:S(2)}) async-start(), calls=%async_computation.15 | async-start | bytes 1990656 | tf_op jit(solution)/shard_map/all_gather | solution.py:43
  809.2 79.5 %all-gather.18.cloned.1.call-start = ((), (), s32[]{:S(2)}) async-start(), calls=%async_computation.13 | async-start | bytes 5971968 | tf_op jit(solution)/shard_map/all_gather | solution.py:43
  809.8 78.9 %all-gather.22.cloned.1.call-start = ((), (), s32[]{:S(2)}) async-start(), calls=%async_computation.17 | async-start | bytes 7520256 | tf_op jit(solution)/shard_map/all_gather | solution.py:43
  810.5 78.2 %all-gather.24.cloned.1.call-start = ((), (), s32[]{:S(2)}) async-start(), calls=%async_computation.19 | async-start | bytes 7520256 | tf_op jit(solution)/shard_map/all_gather | solution.py:43
  811.6 12.4 %copy-start.3 = (bf16[3,2,4,184,288]{3,2,4,1,0:T(4,128)(2,1)S(1)}, bf16[3,2,4,184,288]{3,2,4,1,0:T(4,128)(2,1)}, u32[]{:S(2)}) copy-start(bf16[3,2,4,184,288]{3,2,4,1,0:T(4,128)(2,1)} %copy.97) | copy-start | bytes 7630852
  825.6 10.9 %copy-start.29 = (f32[368]{0:T(512)S(1)}, f32[368]{0:T(512)}, u32[]{:S(2)}) copy-start(f32[368]{0:T(512)} %copy-done.28) | copy-start | bytes 4420
  839.6 46.0 %copy-start.7 = (bf16[2,184,1152]{2,1,0:T(8,128)(2,1)S(1)}, bf16[2,184,1152]{2,1,0:T(8,128)(2,1)}, u32[]{:S(2)}) copy-start(bf16[2,184,1152]{2,1,0:T(8,128)(2,1)} %param.33) | copy-start | bytes 2543620
  888.7 5.6 copy-start.12
  894.3 5.9 copy-start.1
  (34 other events, 106.0 us)
Sparse Core Ops, SparseCore 0:
  10.5 56.7 all-gather.9
  69.2 30.1 all-gather.11
  101.8 61.1 all-gather.13
  165.3 61.1 all-gather.15
  265.5 42.5 reduce-scatter.6
  311.6 79.5 reduce-scatter.10
  394.8 79.5 reduce-scatter.8
  477.9 69.2 reduce-scatter.4
  809.3 7.1 all-gather.19
  817.9 14.5 all-gather.17
  834.6 16.0 all-gather.21
  852.0 16.0 all-gather.23

commit v2 on v1

--- a/solution.py
+++ b/solution.py
@@ -28,19 +28,37 @@
     )
 
 
-def gather_weight(w, axis):
-    half = w.shape[axis] // 2
+def core_swap(x):
+    return lax.ppermute(x, "core", [(0, 1), (1, 0)])
+
+
+def in_core_order(mine, other):
+    first = lax.axis_index("core") == 0
+    return jnp.where(first, mine, other), jnp.where(first, other, mine)
+
+
+def gather_weight(w):
+    rows, cols = w.shape
+    half = rows // 2
+    piece = lax.dynamic_slice_in_dim(w, lax.axis_index("core") * half, half, axis=0)
+    mine = lax.all_gather(piece, "fsdp", axis=0, tiled=False)
+    other = core_swap(mine)
+    first, second = in_core_order(mine, other)
+    return jnp.stack([first, second], axis=1).reshape(-1, cols)
+
+
+def reduce_weight(g):
+    rows, cols = g.shape
+    fsdp = lax.axis_size("fsdp")
+    blocks = g.reshape(fsdp, 2, rows // (2 * fsdp), cols)
     core = lax.axis_index("core")
-    piece = lax.dynamic_slice_in_dim(w, core * half, half, axis=axis)
-    return lax.all_gather(piece, ("fsdp", "core"), axis=axis, tiled=True)
-
-
-def reduce_weight(g, axis):
-    part = lax.psum_scatter(
-        g.astype(jnp.bfloat16), ("fsdp", "core"), scatter_dimension=axis, tiled=True
-    )
-    part = lax.psum(part.astype(jnp.float32), ZAX)
-    return lax.all_gather(part, "core", axis=axis, tiled=True)
+    mine = lax.dynamic_index_in_dim(blocks, core, axis=1, keepdims=False)
+    other = lax.dynamic_index_in_dim(blocks, 1 - core, axis=1, keepdims=False)
+    chip = mine + core_swap(other.astype(jnp.bfloat16)).astype(jnp.float32)
+    part = lax.psum_scatter(chip.astype(jnp.bfloat16), "fsdp", scatter_dimension=0, tiled=True)
+    part = lax.psum(part, ZAX).astype(jnp.float32)
+    first, second = in_core_order(part, core_swap(part))
+    return jnp.concatenate([first[0], second[0]], axis=0)
 
 
 def shards(
@@ -82,10 +100,10 @@
         at += n
     g1, b1, bq, bv, bproj, g2, b2, bup, bdown = full_vectors
 
-    w_qkv = gather_weight(qkv_weight, 0)
-    w_proj = gather_weight(proj_weight, 0)
-    w_up = gather_weight(up_weight, 0)
-    w_down = gather_weight(down_weight, 1)
+    w_qkv = gather_weight(qkv_weight)
+    w_proj = gather_weight(proj_weight)
+    w_up = gather_weight(up_weight)
+    w_down_t = gather_weight(down_weight.T)
 
     flags = slot_flags.astype(f32).reshape(pairs, 2)
     row_flags = lax.dynamic_index_in_dim(flags, zh, axis=1, keepdims=False)
@@ -121,15 +139,15 @@
     gate_in = jnp.dot(second_low, w_up, preferred_element_type=f32) + bup
     active, gelu_back = jax.vjp(gelu_tanh, gate_in)
     active_low = active.astype(bf16)
-    result = hidden + jnp.dot(active_low, w_down, preferred_element_type=f32) + bdown
+    result = hidden + lax.dot_general(active_low, w_down_t, (((1,), (1,)), ((), ())), preferred_element_type=f32) + bdown
     row_flag_rows = jnp.repeat(row_flags, part_rows)[:, None]
     output = (result * row_flag_rows).astype(bf16).reshape(pairs, part_rows, width)
 
     grad_rows = out_grad.reshape(pairs * part_rows, width).astype(f32) * row_flag_rows
     grad_low = grad_rows.astype(bf16)
-    down_weight_grad = jnp.dot(active_low.T, grad_low, preferred_element_type=f32)
+    down_weight_grad_t = jnp.dot(grad_low.T, active_low, preferred_element_type=f32)
     down_bias_grad = jnp.sum(grad_rows, axis=0)
-    grad_active = jnp.dot(grad_low, w_down.T, preferred_element_type=f32)
+    grad_active = jnp.dot(grad_low, w_down_t, preferred_element_type=f32)
     grad_gate = gelu_back(grad_active)[0].astype(bf16)
     up_weight_grad = jnp.dot(second_low.T, grad_gate, preferred_element_type=f32)
     up_bias_grad = jnp.sum(grad_gate.astype(f32), axis=0)
@@ -175,10 +193,10 @@
         at += n
     (n1g, n1b, qb, vb, pb, n2g, n2b, ub, db) = vec_out
 
-    qkv_g = reduce_weight(qkv_weight_grad, 0)
-    proj_g = reduce_weight(proj_weight_grad, 0)
-    up_g = reduce_weight(up_weight_grad, 0)
-    down_g = reduce_weight(down_weight_grad, 1)
+    down_g = reduce_weight(down_weight_grad_t).T
+    up_g = reduce_weight(up_weight_grad)
+    proj_g = reduce_weight(proj_weight_grad)
+    qkv_g = reduce_weight(qkv_weight_grad)
 
     return (output, input_grad, n1g, n1b, qkv_g, qb, vb, proj_g, pb, n2g, n2b, up_g, ub, down_g, db)
 

time: 915 us -> 1020 us (1.11)
  blocking collectives: 368 us -> 61.8 us
  waiting for transfers between devices: 161 us -> 459 us
  other arithmetic: 46.4 us -> 141 us
  local copies, waits for them, and re-layouts: 148 us -> 171 us
  matrix products: 154 us -> 140 us
    psum x1 -> x0, blocking collectives: 262 us -> none  [reduce_weight(): part = lax.psum(part.astype(jnp.float32), ZAX)]
    all_gather x8 -> x4, waiting for transfers between devices: 26.9 us -> 181 us  [gather_weight(): mine = lax.all_gather(piece, 'fsdp', axis=0, tiled=False)]
    psum x0 -> x1, waiting for transfers between devices: none -> 146 us  [reduce_weight(): part = lax.psum(part, ZAX).astype(jnp.float32)]
    unnamed x12 -> x13, waiting for transfers between devices: 1.38 us -> 78.1 us
    reduce_scatter x4 -> x0, waiting for transfers between devices: 74.1 us -> none  [reduce_weight(): lax.psum_scatter(g.astype(jnp.bfloat16), ('fsdp', 'core'), scatter_dimens...]
    another operation x0 -> x8, other arithmetic: none -> 48.9 us  [gather_weight(): return jnp.stack([first, second], axis=1).reshape(-1, cols)]
    all_to_all x1 -> x0, blocking collectives: 43.3 us -> none  [shards(): lax.all_to_all(dqkv, GROUP, split_axis=2, concat_axis=3, tiled=True)]
    convert_element_type x0 -> x9, other arithmetic: none -> 32.3 us  [the longest x4 28.1 us: reduce_weight(): chip.astype(jnp.bfloat16)]
  transfers between devices with their start and end apart: 15 -> 25, of which waited for: 6 -> 10; matrix products, arithmetic and copies ran while one was open for 33% -> 32% of each run, Pallas kernels for 0% -> 0%
where the time goes in v2:
time: 1020 us; the launch traced here: 1010 us
  waiting for transfers between devices  459 us (45%)
  local copies, waits for them, and re-layouts  171 us (17%)
  other arithmetic  141 us (14%)
  matrix products  140 us (14%)
  blocking collectives  61.8 us (6%)
  starting transfers between devices  21.7 us (2%)
  between operations  15.9 us (2%)
    all_gather x4, waiting for transfers between devices, gather_weight(): mine = lax.all_gather(piece, 'fsdp', axis=0, tiled=False)  181 us
    psum x1, waiting for transfers between devices, reduce_weight(): part = lax.psum(part, ZAX).astype(jnp.float32)  146 us
    unnamed x13, waiting for transfers between devices  78.1 us
    another operation x8, other arithmetic, gather_weight(): return jnp.stack([first, second], axis=1).reshape(-1, cols)  48.9 us
    unnamed x2, blocking collectives  34.6 us
    convert_element_type x4, other arithmetic, reduce_weight(): chip.astype(jnp.bfloat16)  28.1 us
    psum x1, blocking collectives, shards(): stacked = lax.psum(stacked, SEQ).reshape(-1)  27.2 us
    all_to_all x1, waiting for transfers between devices, shards(): lax.all_to_all(dqkv, GROUP, split_axis=2, concat_axis=3, tiled=True)  25.1 us
  transfers between devices with their start and end apart: 25, of which 10 were waited for; matrix products, arithmetic and copies ran while one was open for 32% of the time, Pallas kernels for 0%

profile of v2, /device:TPU:0, one launch (start us, length us, event | category | flops | bytes accessed | tf_op | source)
XLA Modules:
  0.0 1009.0 jit_solution(17743258620124356132)
XLA Ops:
  14.5 49.5 %all-gather.10.cloned.1.call-done = bf16[576,3456]{1,0:T(8,128)(2,1)} async-done(((bf16[144,3456]{1,0:T(8,128)(2,1)}), bf16[576,3456]{1,0:T(8,128)(2,1)}) %all-gather.10.cloned.1.call-update) | async-done | bytes 3981328 | tf_op jit(solution)/shard_map/all_gather | solution.py:44
  65.6 16.9 %all-reduce = f32[13520]{0:T(1024)S(1)} all-reduce(f32[13520]{0:T(1024)S(1)} %convert_dynamic-update-slice_fusion), channel_id=2, replica_groups=mesh['zh'=2,'zl'=2,'core'=2,'fsdp'=4] {'fsdp'}, use_global_device_ids=true, to_apply=%add | all-reduce | flops 13520 | bytes 108160
  95.6 61.8 %all-gather.16.cloned.1.call-done = bf16[576,4304]{1,0:T(8,128)(2,1)} async-done(((bf16[144,4304]{1,0:T(8,128)(2,1)}), bf16[576,4304]{1,0:T(8,128)(2,1)}) %all-gather.16.cloned.1.call-update) | async-done | bytes 4958224 | tf_op jit(solution)/shard_map/all_gather | solution.py:44
  157.5 61.7 %all-gather.14.cloned.1.call-done = bf16[576,4304]{1,0:T(8,128)(2,1)} async-done(((bf16[144,4304]{1,0:T(8,128)(2,1)}), bf16[576,4304]{1,0:T(8,128)(2,1)}) %all-gather.14.cloned.1.call-update) | async-done | bytes 4958224 | tf_op jit(solution)/shard_map/all_gather | solution.py:44
  250.5 8.5 pad_maximum_fusion.5
  267.9 8.5 select_bitcast_fusion.1
  284.7 20.6 %all-to-all-done = bf16[3,2,184,1152]{2,1,0,3:T(2,128)(2,1)} async-done(((bf16[3,2,184,1152]{2,1,0,3:T(2,128)(2,1)}), bf16[3,2,184,1152]{2,1,0,3:T(2,128)(2,1)}, u32[]{:S(2)}, u32[]{:S(2)}) %all-to-all-start) | async-done | bytes 2543648 | tf_op jit(solution)/shard_map/all_to_all | solution.py:121
  305.3 12.6 %copy.128 = bf16[3,2,184,4,288]{4,3,2,1,0:T(4,128)(2,1)} copy(bf16[3,2,184,4,288]{2,1,0,4,3:T(2,128)(2,1)} %bitcast.11) | data formatting | bytes 5087232 | tf_op jit(solution)/shard_map/all_to_all | solution.py:121
  339.3 10.7 %fusion.63 = (f32[2,4,736]{2,1,0:T(4,128)S(1)}, f32[2,4,736,736]{2,3,1,0:T(8,128)}) fusion(f32[2,736]{1,0:T(2,128)S(1)} %fusion.49, bf16[2,736,4,72]{1,3,2,0:T(8,128)(2,1)} %squeeze.70, bf16[2,736,4,72]{1,3,2,0:T(8,128)(2,1)S(1)} %squeeze.71), kind=kOutput, calls=%fused_computation.161 | convolution fusion | flops 641368768 | bytes 19059456 | tf_op jit(solution)/shard_map/sub | solution.py:128
  350.0 9.1 fusion.34
  368.0 8.7 pad_maximum_fusion
  376.7 8.3 copy.99
  385.1 8.6 pad_maximum_fusion.1
  403.0 8.4 convolution_add_fusion
  411.5 10.7 %convert_reduce_fusion = (f32[4304]{0:T(1024)}, bf16[368,4304]{1,0:T(8,128)(2,1)}) fusion(f32[368,4304]{1,0:T(8,128)S(1)} %convolution_add_fusion, bf16[368,1152]{1,0:T(8,128)(2,1)S(1)} %bitcast.232, bf16[1152,4304]{1,0:T(8,128)(2,1)S(1)} %bitcast.202), kind=kOutput, calls=%fused_computation.32 | convolution fusion | flops 3690417408 | bytes 20284736 | tf_op jit(solution)/shard_map/dot_general | solution.py:150
  422.2 10.1 multiply_reduce_fusion.1
  432.2 10.0 fusion.54
  478.7 12.3 %multiply_reduce_fusion = (f32[2,4,736]{2,1,0:T(4,128)S(1)}, f32[2,4,736,736]{2,3,1,0:T(8,128)}) fusion(f32[2,4,736,736]{2,3,1,0:T(8,128)} %get-tuple-element.83, f32[2,4,736]{2,1,0:T(4,128)S(1)} %get-tuple-element.82, bf16[2,736,4,72]{1,3,2,0:T(8,128)(2,1)} %reshape.304, bf16[2,736,4,72]{1,3,2,0:T(8,128)(2,1)} %squeeze.69), kind=kOutput, calls=%fused_computation.2 | convolution fusion | flops 637028608 | bytes 36411392 | tf_op jit(solution)/shard_map/pqhd,pkhd->phqk/dot_general | solution.py:165
  490.9 12.3 %multiply_convert_fusion = bf16[2,4,736,736]{2,3,1,0:T(8,128)(2,1)S(1)} fusion(f32[2,4,736,736]{2,3,1,0:T(8,128)} %get-tuple-element.88, f32[2,4,736]{2,1,0:T(4,128)S(1)} %get-tuple-element.87, f32[2,4,736,736]{2,3,1,0:T(8,128)} %get-tuple-element.83, f32[2,4,736]{2,1,0:T(4,128)S(1)} %get-tuple-element.82), kind=kLoop, calls=%fused_computation.1 | loop fusion | flops 17334272 | bytes 43382784 | tf_op jit(solution)/shard_map/convert_element_type | solution.py:167
  503.3 9.9 fusion.37
  531.8 8.7 pad_maximum_fusion.6
  548.8 8.7 fusion.3
  559.7 25.1 %all-to-all-done.3 = bf16[3,2,736,288]{3,1,0,2:T(2,128)(2,1)} async-done(((bf16[3,2,736,288]{3,1,0,2:T(2,128)(2,1)}), bf16[3,2,736,288]{3,1,0,2:T(2,128)(2,1)}, u32[]{:S(2)}, u32[]{:S(2)}) %all-to-all-start.3) | async-done | bytes 2543648 | tf_op jit(solution)/shard_map/all_to_all | solution.py:172
  584.8 12.9 %copy.133 = bf16[3,2,4,184,288]{3,2,4,1,0:T(4,128)(2,1)} copy(bf16[3,2,4,184,288]{4,1,0,3,2:T(2,128)(2,1)} %bitcast.47) | data formatting | bytes 5087232 | tf_op jit(solution)/shard_map/all_to_all | solution.py:172
  664.1 12.5 %fusion.20 = f32[4,2,144,4304]{3,2,1,0:T(8,128)} fusion(bf16[4,2,144,368]{3,2,1,0:T(8,128)(2,1)S(1)} %bitcast.207, f32[368,4304]{1,0:T(8,128)} %copy-done.13), kind=kOutput, calls=%fused_computation.52 | convolution fusion | flops 3663495936 | bytes 27016192 | tf_op jit(solution)/shard_map/dot_general | solution.py:148
  690.2 8.9 fusion.2
  699.4 14.9 %reduce-scatter.13.cloned.1.call-done = bf16[1,144,3456]{2,1,0:T(8,128)(2,1)} async-done(((bf16[4,144,3456]{2,1,0:T(8,128)(2,1)}), bf16[1,144,3456]{2,1,0:T(8,128)(2,1)}) %reduce-scatter.13.cloned.1.call-update) | async-done | bytes 995344
  714.3 63.1 %reduce-scatter.19.cloned.1.call-done = bf16[1,144,4304]{2,1,0:T(8,128)(2,1)} async-done(((bf16[4,144,4304]{2,1,0:T(8,128)(2,1)}), bf16[1,144,4304]{2,1,0:T(8,128)(2,1)}) %reduce-scatter.19.cloned.1.call-update) | async-done | bytes 1239568
  777.6 145.9 %all-reduce.9.cloned.1.call-done = (bf16[1,144,3456]{2,1,0:T(8,128)(2,1)}, bf16[1,144,1152]{2,1,0:T(8,128)(2,1)}, bf16[1,144,4304]{2,1,0:T(8,128)(2,1)}, bf16[1,144,4304]{2,1,0:T(8,128)(2,1)}) async-done(((bf16[1,144,3456]{2,1,0:T(8,128)(2,1)}, bf16[1,144,1152]{2,1,0:T(8,128)(2,1)}, bf16[1,144,4304]{2,1,0:T(8,128)(2,1)}, bf16[1,144,4304]{2,1,0:T(8,128)(2,1)}), (bf16[1,144,3456]{2,1,0:T(8,128)(2,1)}, ...) | async-done | bytes 3806224 | tf_op jit(solution)/shard_map/psum | solution.py:59
  926.1 11.2 %fusion.25 = bf16[368,1152]{1,0:T(8,128)(2,1)} fusion(f32[368,1152]{1,0:T(8,128)S(1)} %copy-done.6, bf16[1152,4304]{1,0:T(8,128)(2,1)} %bitcast.199, f32[368]{0:T(512)S(1)} %mul.257, f32[1152]{0:T(1024)S(1)} %add.220, f32[368,4304]{1,0:T(8,128)} %copy-done.13), kind=kOutput, calls=%fused_computation.59 | convolution fusion | flops 3665191680 | bytes 18801600 | tf_op jit(solution)/shard_map/dot_general | solution.py:142
  941.0 17.7 %all-reduce.1 = f32[4,3380]{1,0:T(4,128)} all-reduce(f32[4,3380]{1,0:T(4,128)S(1)} %concatenate.26), channel_id=7, replica_groups=mesh['zh'=2,'zl'=2,'core'=2,'fsdp'=4] {'fsdp'}, use_global_device_ids=true, to_apply=%region_20.21.clone | all-reduce | flops 13520 | bytes 108160
  961.1 27.2 %psum.35 = f32[1,3380]{1,0:T(1,128)S(1)} all-reduce(f32[1,3380]{1,0:T(1,128)S(1)} %constant_dynamic-slice_fusion.5), channel_id=1, replica_groups=mesh['zh'=2,'zl'=2,'core'=2,'fsdp'=4] {'zh','zl','core'}, use_global_device_ids=true, to_apply=%region_21.22 | all-reduce | flops 3380 | bytes 27040 | tf_op jit(solution)/shard_map/psum | solution.py:187
  (300 shorter events, 277.4 us)
Async XLA Ops:
  7.2 56.8 %all-gather.10.cloned.1.call-start = ((), (), s32[]{:S(2)}) async-start(), calls=%async_computation.8 | async-start | bytes 4976640 | tf_op jit(solution)/shard_map/all_gather | solution.py:44
  9.7 85.9 %all-gather.12.cloned.1.call-start = ((), (), s32[]{:S(2)}) async-start(), calls=%async_computation.9 | async-start | bytes 1658880 | tf_op jit(solution)/shard_map/all_gather | solution.py:44
  10.5 146.9 %all-gather.16.cloned.1.call-start = ((), (), s32[]{:S(2)}) async-start(), calls=%async_computation.11 | async-start | bytes 6266880 | tf_op jit(solution)/shard_map/all_gather | solution.py:44
  11.8 71.9 %copy-start.55 = (s32[4]{0:T(128)S(1)}, s32[4]{0:T(128)}, u32[]{:S(2)}) copy-start(s32[4]{0:T(128)} %param.19) | copy-start | bytes 52
  11.8 72.6 %copy-start.3 = (bf16[2,184,1152]{2,1,0:T(8,128)(2,1)S(1)}, bf16[2,184,1152]{2,1,0:T(8,128)(2,1)}, u32[]{:S(2)}) copy-start(bf16[2,184,1152]{2,1,0:T(8,128)(2,1)} %param.17) | copy-start | bytes 2543620
  11.9 73.8 %copy-start.9 = (bf16[2,184,1152]{2,1,0:T(8,128)(2,1)S(1)}, bf16[2,184,1152]{2,1,0:T(8,128)(2,1)}, u32[]{:S(2)}) copy-start(bf16[2,184,1152]{2,1,0:T(8,128)(2,1)} %param.33) | copy-start | bytes 2543620
  11.9 207.3 %all-gather.14.cloned.1.call-start = ((), (), s32[]{:S(2)}) async-start(), calls=%async_computation.10 | async-start | bytes 6266880 | tf_op jit(solution)/shard_map/all_gather | solution.py:44
  64.0 155.2 %collective-permute-start = (bf16[4,144,3456]{2,1,0:T(8,128)(2,1)}, bf16[4,144,3456]{2,1,0:T(8,128)(2,1)}, u32[]{:S(2)}, u32[]{:S(2)}) collective-permute-start(bf16[4,144,3456]{2,1,0:T(8,128)(2,1)} %bitcast.215), channel_id=1, source_target_pairs={{0,4},{4,0},{1,5},{5,1},{2,6},{6,2},{3,7},{7,3},{8,12},{12,8},{9,1... | collective-permute-start | bytes 11943944 | tf_op jit(solution)/shard_map/ppermute | solution.py:32
  84.7 139.5 %copy-start.36 = (f32[2,184]{1,0:T(2,128)}, f32[2,184]{1,0:T(2,128)S(1)}, u32[]{:S(2)}) copy-start(f32[2,184]{1,0:T(2,128)S(1)} %broadcast_multiply_fusion.1) | copy-start | bytes 4420
  95.6 168.5 %collective-permute-start.1 = (bf16[4,144,1152]{2,1,0:T(8,128)(2,1)}, bf16[4,144,1152]{2,1,0:T(8,128)(2,1)}, u32[]{:S(2)}, u32[]{:S(2)}) collective-permute-start(bf16[4,144,1152]{2,1,0:T(8,128)(2,1)} %bitcast.228), channel_id=1, source_target_pairs={{0,4},{4,0},{1,5},{5,1},{2,6},{6,2},{3,7},{7,3},{8,12},{12,8},{9,1... | collective-permute-start | bytes 3981320 | tf_op jit(solution)/shard_map/ppermute | solution.py:32
  157.5 110.4 %collective-permute-start.3 = (bf16[4,144,4304]{2,1,0:T(8,128)(2,1)}, bf16[4,144,4304]{2,1,0:T(8,128)(2,1)}, u32[]{:S(2)}, u32[]{:S(2)}) collective-permute-start(bf16[4,144,4304]{2,1,0:T(8,128)(2,1)} %bitcast.209), channel_id=1, source_target_pairs={{0,4},{4,0},{1,5},{5,1},{2,6},{6,2},{3,7},{7,3},{8,12},{12,8},{9,1... | collective-permute-start | bytes 14874632 | tf_op jit(solution)/shard_map/ppermute | solution.py:32
  219.2 57.2 %collective-permute-start.2 = (bf16[4,144,4304]{2,1,0:T(8,128)(2,1)}, bf16[4,144,4304]{2,1,0:T(8,128)(2,1)}, u32[]{:S(2)}, u32[]{:S(2)}) collective-permute-start(bf16[4,144,4304]{2,1,0:T(8,128)(2,1)} %bitcast.211), channel_id=1, source_target_pairs={{0,4},{4,0},{1,5},{5,1},{2,6},{6,2},{3,7},{7,3},{8,12},{12,8},{9,1... | collective-permute-start | bytes 14874632 | tf_op jit(solution)/shard_map/ppermute | solution.py:32
  258.9 46.3 %all-to-all-start = ((bf16[3,2,184,1152]{2,1,0,3:T(2,128)(2,1)}), bf16[3,2,184,1152]{2,1,0,3:T(2,128)(2,1)}, u32[]{:S(2)}, u32[]{:S(2)}) async-start(bf16[3,2,184,1152]{2,1,0,3:T(2,128)(2,1)} %pad_maximum_fusion.5), calls=%async_computation | async-start | bytes 7077888 | tf_op jit(solution)/shard_map/all_to_all | solution.py:121
  363.7 29.9 %all-to-all-start.1 = ((bf16[2,736,288]{2,0,1:T(2,128)(2,1)}), bf16[2,736,288]{2,0,1:T(2,128)(2,1)}, u32[]{:S(2)}, u32[]{:S(2)}) async-start(bf16[2,736,288]{2,0,1:T(2,128)(2,1)} %copy.95), calls=%async_computation.1 | async-start | bytes 2260992 | tf_op jit(solution)/shard_map/all_to_all | solution.py:133
  451.6 20.6 %all-to-all-start.2 = ((bf16[2,184,1152]{1,0,2:T(2,128)(2,1)}), bf16[2,184,1152]{1,0,2:T(2,128)(2,1)}, u32[]{:S(2)}, u32[]{:S(2)}) async-start(bf16[2,184,1152]{1,0,2:T(2,128)(2,1)} %copy.101), calls=%async_computation.2 | async-start | bytes 2359296 | tf_op jit(solution)/shard_map/all_to_all | solution.py:161
  465.1 80.2 %collective-permute-start.6 = (bf16[4,144,1152]{2,1,0:T(8,128)(2,1)}, bf16[4,144,1152]{2,1,0:T(8,128)(2,1)}, u32[]{:S(2)}, u32[]{:S(2)}) collective-permute-start(bf16[4,144,1152]{2,1,0:T(8,128)(2,1)} %fusion.40), channel_id=1, source_target_pairs={{0,4},{4,0},{1,5},{5,1},{2,6},{6,2},{3,7},{7,3},{8,12},{12,8},{9,1... | collective-permute-start | bytes 3981320 | tf_op jit(solution)/shard_map/ppermute | solution.py:32
  472.2 76.7 %collective-permute-start.8 = (bf16[4,144,4304]{2,1,0:T(8,128)(2,1)}, bf16[4,144,4304]{2,1,0:T(8,128)(2,1)}, u32[]{:S(2)}, u32[]{:S(2)}) collective-permute-start(bf16[4,144,4304]{2,1,0:T(8,128)(2,1)} %fusion.13), channel_id=1, source_target_pairs={{0,4},{4,0},{1,5},{5,1},{2,6},{6,2},{3,7},{7,3},{8,12},{12,8},{9,1... | collective-permute-start | bytes 14874632 | tf_op jit(solution)/shard_map/ppermute | solution.py:32
  540.5 44.3 %all-to-all-start.3 = ((bf16[3,2,736,288]{3,1,0,2:T(2,128)(2,1)}), bf16[3,2,736,288]{3,1,0,2:T(2,128)(2,1)}, u32[]{:S(2)}, u32[]{:S(2)}) async-start(bf16[3,2,736,288]{3,1,0,2:T(2,128)(2,1)} %pad_maximum_fusion.6), calls=%async_computation.3 | async-start | bytes 6782976 | tf_op jit(solution)/shard_map/all_to_all | solution.py:172
  545.2 154.2 %reduce-scatter.15.cloned.1.call-start = ((), (), s32[]{:S(2)}) async-start(), calls=%async_computation.13 | async-start | bytes 1658880
  548.8 150.6 %reduce-scatter.17.cloned.1.call-start = ((), (), s32[]{:S(2)}) async-start(), calls=%async_computation.14 | async-start | bytes 6266880
  557.5 156.8 %reduce-scatter.13.cloned.1.call-start = ((), (), s32[]{:S(2)}) async-start(), calls=%async_computation.12 | async-start | bytes 4976640
  648.2 8.7 collective-permute-start.4
  664.0 113.4 %reduce-scatter.19.cloned.1.call-start = ((), (), s32[]{:S(2)}) async-start(), calls=%async_computation.15 | async-start | bytes 6266880
  681.1 9.1 collective-permute-start.10
  699.1 78.4 %copy-start.39 = (f32[4,288]{1,0:T(4,128)S(1)}, f32[4,288]{1,0:T(4,128)}, u32[]{:S(2)}) copy-start(f32[4,288]{1,0:T(4,128)} %get-tuple-element.71) | copy-start | bytes 13828
  699.1 78.4 %copy-start.35 = (f32[1152]{0:T(1024)S(1)}, f32[1152]{0:T(1024)}, u32[]{:S(2)}) copy-start(f32[1152]{0:T(1024)} %get-tuple-element.68) | copy-start | bytes 13828
  699.1 224.3 %all-reduce.9.cloned.1.call-start = ((), (), s32[]{:S(2)}) async-start(), calls=%async_computation.16 | async-start | bytes 7667712 | tf_op jit(solution)/shard_map/psum | solution.py:59
  777.4 148.8 %copy-start.6 = (f32[368,1152]{1,0:T(8,128)S(1)}, f32[368,1152]{1,0:T(8,128)}, u32[]{:S(2)}) copy-start(f32[368,1152]{1,0:T(8,128)} %copy-done.5) | copy-start | bytes 5087236
  926.1 65.9 %collective-permute-start.5 = (f32[1,144,3456]{2,1,0:T(8,128)}, f32[1,144,3456]{2,1,0:T(8,128)}, u32[]{:S(2)}, u32[]{:S(2)}) collective-permute-start(f32[1,144,3456]{2,1,0:T(8,128)} %convert_element_type.225), channel_id=1, source_target_pairs={{0,4},{4,0},{1,5},{5,1},{2,6},{6,2},{3,7},{7,3},{8,12},{12,8},{9,1... | collective-permute-start | bytes 5971976 | tf_op jit(solution)/shard_map/ppermute | solution.py:32
  959.7 31.0 %collective-permute-start.7 = (f32[1,144,1152]{2,1,0:T(8,128)}, f32[1,144,1152]{2,1,0:T(8,128)S(1)}, u32[]{:S(2)}, u32[]{:S(2)}) collective-permute-start(f32[1,144,1152]{2,1,0:T(8,128)} %convert_element_type.230), channel_id=1, source_target_pairs={{0,4},{4,0},{1,5},{5,1},{2,6},{6,2},{3,7},{7,3},{8,12},{12,8},{9,1... | collective-permute-start | bytes 1990664 | tf_op jit(solution)/shard_map/ppermute | solution.py:32
  989.9 6.1 collective-permute-start.9
  990.1 8.8 collective-permute-start.11
  (52 other events, 982.3 us)
Sparse Core Ops, SparseCore 0:
  10.4 53.5 all-gather.9
  66.4 29.1 all-gather.11
  98.1 59.3 all-gather.15
  159.7 59.3 all-gather.13
  549.3 30.3 reduce-scatter.14
  583.3 59.4 reduce-scatter.16
  664.1 50.1 reduce-scatter.12
  717.9 59.4 reduce-scatter.18
  780.0 143.3 all-reduce.8

commit v3 on v2

--- a/solution.py
+++ b/solution.py
@@ -38,13 +38,9 @@
 
 
 def gather_weight(w):
-    rows, cols = w.shape
-    half = rows // 2
+    half = w.shape[0] // 2
     piece = lax.dynamic_slice_in_dim(w, lax.axis_index("core") * half, half, axis=0)
-    mine = lax.all_gather(piece, "fsdp", axis=0, tiled=False)
-    other = core_swap(mine)
-    first, second = in_core_order(mine, other)
-    return jnp.stack([first, second], axis=1).reshape(-1, cols)
+    return lax.all_gather(piece, ("fsdp", "core"), axis=0, tiled=True)
 
 
 def reduce_weight(g):
@@ -193,10 +189,14 @@
         at += n
     (n1g, n1b, qb, vb, pb, n2g, n2b, ub, db) = vec_out
 
-    down_g = reduce_weight(down_weight_grad_t).T
+    down_g = reduce_weight(down_weight_grad_t)
+    up_weight_grad, down_g = lax.optimization_barrier((up_weight_grad, down_g))
     up_g = reduce_weight(up_weight_grad)
+    proj_weight_grad, up_g = lax.optimization_barrier((proj_weight_grad, up_g))
     proj_g = reduce_weight(proj_weight_grad)
+    qkv_weight_grad, proj_g = lax.optimization_barrier((qkv_weight_grad, proj_g))
     qkv_g = reduce_weight(qkv_weight_grad)
+    down_g = down_g.T
 
     return (output, input_grad, n1g, n1b, qkv_g, qb, vb, proj_g, pb, n2g, n2b, up_g, ub, down_g, db)
 

time: 1020 us -> 1020 us (level)
  other arithmetic: 141 us -> 98.7 us
  waiting for transfers between devices: 459 us -> 480 us
  local copies, waits for them, and re-layouts: 171 us -> 182 us
    all_gather x4, waiting for transfers between devices: 181 us -> 88.7 us  [gather_weight(): return lax.all_gather(piece, ('fsdp', 'core'), axis=0, tiled=True)]
    another operation x8 -> x0, other arithmetic: 48.9 us -> none  [gather_weight(): return jnp.stack([first, second], axis=1).reshape(-1, cols)]
    psum x1 -> x4, waiting for transfers between devices: 146 us -> 172 us  [reduce_weight(): part = lax.psum(part, ZAX).astype(jnp.float32)]
    optimization_barrier x0 -> x1, local copies, waits for them, and re-layouts: none -> 21.7 us  [shards(): up_weight_grad, down_g = lax.optimization_barrier((up_weight_grad, down_g))]
    all_to_all x1, waiting for transfers between devices: 20.6 us -> 41.1 us  [shards(): lax.all_to_all(qkv_tok, GROUP, split_axis=3, concat_axis=2, tiled=True)]
    unnamed x13 -> x16, waiting for transfers between devices: 78.1 us -> 97.9 us
    ppermute x12 -> x8, waiting for transfers between devices: 8.12 us -> 23.4 us  [core_swap(): return lax.ppermute(x, 'core', [(0, 1), (1, 0)])]
    all_to_all x1, waiting for transfers between devices: 25.1 us -> 36 us  [shards(): lax.all_to_all(dqkv, GROUP, split_axis=2, concat_axis=3, tiled=True)]
  transfers between devices with their start and end apart: 25 -> 24, of which waited for: 10 -> 16; matrix products, arithmetic and copies ran while one was open for 32% -> 31% of each run, Pallas kernels for 0% -> 0%
where the time goes in v3:
time: 1020 us; the launch traced here: 1010 us
  waiting for transfers between devices  480 us (47%)
  local copies, waits for them, and re-layouts  182 us (18%)
  matrix products  149 us (15%)
  other arithmetic  98.7 us (10%)
  blocking collectives  63 us (6%)
  starting transfers between devices  20.5 us (2%)
  between operations  15.9 us (2%)
    psum x4, waiting for transfers between devices, reduce_weight(): part = lax.psum(part, ZAX).astype(jnp.float32)  172 us
    unnamed x16, waiting for transfers between devices  97.9 us
    all_gather x4, waiting for transfers between devices, gather_weight(): return lax.all_gather(piece, ('fsdp', 'core'), axis=0, tiled=True)  88.7 us
    all_to_all x1, waiting for transfers between devices, shards(): lax.all_to_all(qkv_tok, GROUP, split_axis=3, concat_axis=2, tiled=True)  41.1 us
    unnamed x2, blocking collectives  37.1 us
    all_to_all x1, waiting for transfers between devices, shards(): lax.all_to_all(dqkv, GROUP, split_axis=2, concat_axis=3, tiled=True)  36 us
    convert_element_type x4, other arithmetic, reduce_weight(): chip.astype(jnp.bfloat16)  26.9 us
    psum x1, blocking collectives, shards(): stacked = lax.psum(stacked, SEQ).reshape(-1)  25.9 us
  transfers between devices with their start and end apart: 24, of which 16 were waited for; matrix products, arithmetic and copies ran while one was open for 31% of the time, Pallas kernels for 0%

profile of v3, /device:TPU:0, one launch (start us, length us, event | category | flops | bytes accessed | tf_op | source)
XLA Modules:
  0.0 1008.7 jit_solution(4872745844127084546)
XLA Ops:
  14.5 20.1 %all-reduce = f32[13520]{0:T(1024)S(1)} all-reduce(f32[13520]{0:T(1024)S(1)} %convert_dynamic-update-slice_fusion), channel_id=2, replica_groups=mesh['zh'=2,'zl'=2,'core'=2,'fsdp'=4] {'fsdp'}, use_global_device_ids=true, to_apply=%add | all-reduce | flops 13520 | bytes 108160
  38.0 28.6 %all-gather.6.cloned.1.call-done = bf16[1152,3456]{1,0:T(8,128)(2,1)} async-done(((bf16[144,3456]{1,0:T(8,128)(2,1)}), bf16[1152,3456]{1,0:T(8,128)(2,1)}) %all-gather.6.cloned.1.call-update) | async-done | bytes 7962640 | tf_op jit(solution)/shard_map/all_gather | solution.py:43
  97.4 41.1 %all-to-all-done = bf16[3,2,184,1152]{2,1,0,3:T(2,128)(2,1)} async-done(((bf16[3,2,184,1152]{2,1,0,3:T(2,128)(2,1)}), bf16[3,2,184,1152]{2,1,0,3:T(2,128)(2,1)}, u32[]{:S(2)}, u32[]{:S(2)}) %all-to-all-start) | async-done | bytes 2543648 | tf_op jit(solution)/shard_map/all_to_all | solution.py:117
  138.5 12.6 %copy.112 = bf16[3,2,184,4,288]{4,3,2,1,0:T(4,128)(2,1)} copy(bf16[3,2,184,4,288]{2,1,0,4,3:T(2,128)(2,1)} %bitcast.5) | data formatting | bytes 5087232 | tf_op jit(solution)/shard_map/all_to_all | solution.py:117
  169.2 10.8 %fusion.55 = (f32[2,4,736]{2,1,0:T(4,128)S(1)}, f32[2,4,736,736]{2,3,1,0:T(8,128)}) fusion(f32[2,736]{1,0:T(2,128)S(1)} %fusion.42, bf16[2,736,4,72]{1,3,2,0:T(8,128)(2,1)} %squeeze.70, bf16[2,736,4,72]{1,3,2,0:T(8,128)(2,1)S(1)} %squeeze.71), kind=kOutput, calls=%fused_computation.140 | convolution fusion | flops 641368768 | bytes 19059456 | tf_op jit(solution)/shard_map/sub | solution.py:124
  179.9 8.8 fusion.30
  201.9 10.4 %all-to-all-done.1 = bf16[2,736,288]{2,0,1:T(2,128)(2,1)S(1)} async-done(((bf16[2,736,288]{2,0,1:T(2,128)(2,1)}), bf16[2,736,288]{2,0,1:T(2,128)(2,1)S(1)}, u32[]{:S(2)}, u32[]{:S(2)}) %all-to-all-start.1) | async-done | bytes 847904 | tf_op jit(solution)/shard_map/all_to_all | solution.py:129
  230.7 9.7 fusion.20
  247.0 8.7 collective-permute-done
  255.6 8.6 fusion.3
  264.3 58.6 %reduce-scatter.13.cloned.1.call-done = bf16[1,144,4304]{2,1,0:T(8,128)(2,1)} async-done(((bf16[4,144,4304]{2,1,0:T(8,128)(2,1)}), bf16[1,144,4304]{2,1,0:T(8,128)(2,1)}) %reduce-scatter.13.cloned.1.call-update) | async-done | bytes 1239568
  326.0 58.0 %all-reduce.11.cloned.1.call-done = bf16[1,144,4304]{2,1,0:T(8,128)(2,1)} async-done(((bf16[1,144,4304]{2,1,0:T(8,128)(2,1)}), bf16[1,144,4304]{2,1,0:T(8,128)(2,1)}) %all-reduce.11.cloned.1.call-update) | async-done | bytes 1239568 | tf_op jit(solution)/shard_map/psum | solution.py:55
  386.9 60.2 %all-gather.12.cloned.1.call-done = bf16[1152,4304]{1,0:T(8,128)(2,1)} async-done(((bf16[144,4304]{1,0:T(8,128)(2,1)}), bf16[1152,4304]{1,0:T(8,128)(2,1)}) %all-gather.12.cloned.1.call-update) | async-done | bytes 9916432 | tf_op jit(solution)/shard_map/all_gather | solution.py:43
  447.1 11.9 %convert_reduce_fusion = (f32[4304]{0:T(1024)S(1)}, bf16[368,4304]{1,0:T(8,128)(2,1)S(1)}) fusion(f32[368,4304]{1,0:T(8,128)} %copy-done.11, bf16[368,1152]{1,0:T(8,128)(2,1)S(1)} %copy-done.19, bf16[1152,4304]{1,0:T(8,128)(2,1)} %all-gather.12.cloned.1.call-done), kind=kOutput, calls=%fused_computation.29 | convolution fusion | flops 3690417408 | bytes 20284736 | tf_op jit(solution)/shard_map/dot_general | solution.py:146
  459.0 9.9 fusion.46
  473.5 21.7 %copy.104 = f32[1152,4304]{1,0:T(8,128)} copy(f32[1152,4304]{0,1:T(8,128)} %fusion.46) | data formatting | bytes 39665664 | tf_op jit(solution)/shard_map/optimization_barrier | solution.py:193
  508.1 8.6 fusion.2
  516.8 9.3 multiply_reduce_fusion.2
  545.7 10.1 %all-to-all-done.2 = bf16[2,184,1152]{1,0,2:T(2,128)(2,1)} async-done(((bf16[2,184,1152]{1,0,2:T(2,128)(2,1)}), bf16[2,184,1152]{1,0,2:T(2,128)(2,1)}, u32[]{:S(2)}, u32[]{:S(2)}) %all-to-all-start.2) | async-done | bytes 847904 | tf_op jit(solution)/shard_map/all_to_all | solution.py:157
  562.6 12.9 %multiply_reduce_fusion = (f32[2,4,736]{2,1,0:T(4,128)S(1)}, f32[2,4,736,736]{2,3,1,0:T(8,128)}) fusion(f32[2,4,736,736]{2,3,1,0:T(8,128)} %get-tuple-element.78, f32[2,4,736]{2,1,0:T(4,128)S(1)} %get-tuple-element.77, bf16[2,736,4,72]{1,3,2,0:T(8,128)(2,1)} %reshape.263, bf16[2,736,4,72]{1,3,2,0:T(8,128)(2,1)} %squeeze.69), kind=kOutput, calls=%fused_computation.2 | convolution fusion | flops 637028608 | bytes 36411392 | tf_op jit(solution)/shard_map/pqhd,pkhd->phqk/dot_general | solution.py:161
  576.4 16.3 %multiply_convert_fusion = bf16[2,4,736,736]{2,3,1,0:T(8,128)(2,1)} fusion(f32[2,4,736,736]{2,3,1,0:T(8,128)} %get-tuple-element.83, f32[2,4,736]{2,1,0:T(4,128)S(1)} %get-tuple-element.82, f32[2,4,736,736]{2,3,1,0:T(8,128)} %get-tuple-element.78, f32[2,4,736]{2,1,0:T(4,128)S(1)} %get-tuple-element.77), kind=kLoop, calls=%fused_computation.1 | loop fusion | flops 17334272 | bytes 43382784 | tf_op jit(solution)/shard_map/convert_element_type | solution.py:163
  592.7 44.8 %all-reduce.13.cloned.1.call-done = bf16[1,144,4304]{2,1,0:T(8,128)(2,1)} async-done(((bf16[1,144,4304]{2,1,0:T(8,128)(2,1)}), bf16[1,144,4304]{2,1,0:T(8,128)(2,1)}) %all-reduce.13.cloned.1.call-update) | async-done | bytes 1239568 | tf_op jit(solution)/shard_map/psum | solution.py:55
  640.5 9.8 fusion.33
  702.3 36.0 %all-to-all-done.3 = bf16[3,2,736,288]{3,1,0,2:T(2,128)(2,1)} async-done(((bf16[3,2,736,288]{3,1,0,2:T(2,128)(2,1)}), bf16[3,2,736,288]{3,1,0,2:T(2,128)(2,1)}, u32[]{:S(2)}, u32[]{:S(2)}) %all-to-all-start.3) | async-done | bytes 2543648 | tf_op jit(solution)/shard_map/all_to_all | solution.py:168
  738.3 13.3 %copy.117 = bf16[3,2,4,184,288]{3,2,4,1,0:T(4,128)(2,1)} copy(bf16[3,2,4,184,288]{4,1,0,3,2:T(2,128)(2,1)} %bitcast.26) | data formatting | bytes 5087232 | tf_op jit(solution)/shard_map/all_to_all | solution.py:168
  783.2 24.6 %all-reduce.15.cloned.1.call-done = bf16[1,144,1152]{2,1,0:T(8,128)(2,1)} async-done(((bf16[1,144,1152]{2,1,0:T(8,128)(2,1)}), bf16[1,144,1152]{2,1,0:T(8,128)(2,1)}) %all-reduce.15.cloned.1.call-update) | async-done | bytes 331792 | tf_op jit(solution)/shard_map/psum | solution.py:55
  836.5 11.7 %fusion.25 = bf16[368,1152]{1,0:T(8,128)(2,1)} fusion(f32[368,1152]{1,0:T(8,128)S(1)} %get-tuple-element.80, bf16[1152,4304]{1,0:T(8,128)(2,1)} %all-gather.12.cloned.1.call-done, f32[368]{0:T(512)S(1)} %mul.246, f32[1152]{0:T(1024)S(1)} %add.215, f32[368,4304]{1,0:T(8,128)} %copy-done.11), kind=kOutput, calls=%fused_computation.50 | convolution fusion | flops 3665191680 | bytes 18801600 | tf_op jit(solution)/shard_map/dot_general | solution.py:138
  848.1 38.3 %reduce-scatter.19.cloned.1.call-done = bf16[1,144,3456]{2,1,0:T(8,128)(2,1)} async-done(((bf16[4,144,3456]{2,1,0:T(8,128)(2,1)}), bf16[1,144,3456]{2,1,0:T(8,128)(2,1)}) %reduce-scatter.19.cloned.1.call-update) | async-done | bytes 995344
  886.5 8.2 fusion.47
  894.8 44.6 %all-reduce.17.cloned.1.call-done = bf16[1,144,3456]{2,1,0:T(8,128)(2,1)} async-done(((bf16[1,144,3456]{2,1,0:T(8,128)(2,1)}), bf16[1,144,3456]{2,1,0:T(8,128)(2,1)}) %all-reduce.17.cloned.1.call-update) | async-done | bytes 995344 | tf_op jit(solution)/shard_map/psum | solution.py:55
  948.8 17.1 %all-reduce.1 = f32[4,3380]{1,0:T(4,128)S(1)} all-reduce(f32[4,3380]{1,0:T(4,128)S(1)} %concatenate.26), channel_id=3, replica_groups=mesh['zh'=2,'zl'=2,'core'=2,'fsdp'=4] {'fsdp'}, use_global_device_ids=true, to_apply=%region_20.21.clone | all-reduce | flops 13520 | bytes 108160
  966.5 25.9 %psum.35 = f32[1,3380]{1,0:T(1,128)S(1)} all-reduce(f32[1,3380]{1,0:T(1,128)S(1)} %constant_dynamic-slice_fusion.5), channel_id=1, replica_groups=mesh['zh'=2,'zl'=2,'core'=2,'fsdp'=4] {'zh','zl','core'}, use_global_device_ids=true, to_apply=%region_21.22 | all-reduce | flops 3380 | bytes 27040 | tf_op jit(solution)/shard_map/psum | solution.py:183
  (269 shorter events, 281.7 us)
Async XLA Ops:
  7.2 59.4 %all-gather.6.cloned.1.call-start = ((), (), s32[]{:S(2)}) async-start(), calls=%async_computation.8 | async-start | bytes 8957952 | tf_op jit(solution)/shard_map/all_gather | solution.py:43
  9.8 206.7 %all-gather.8.cloned.1.call-start = ((), (), s32[]{:S(2)}) async-start(), calls=%async_computation.9 | async-start | bytes 2985984 | tf_op jit(solution)/shard_map/all_gather | solution.py:43
  11.7 208.6 %all-gather.10.cloned.1.call-start = ((), (), s32[]{:S(2)}) async-start(), calls=%async_computation.10 | async-start | bytes 11280384 | tf_op jit(solution)/shard_map/all_gather | solution.py:43
  35.0 37.6 %copy-start.30 = (f32[368]{0:T(512)}, f32[368]{0:T(512)S(1)}, u32[]{:S(2)}) copy-start(f32[368]{0:T(512)S(1)} %div.47) | copy-start | bytes 4420
  92.2 46.3 %all-to-all-start = ((bf16[3,2,184,1152]{2,1,0,3:T(2,128)(2,1)}), bf16[3,2,184,1152]{2,1,0,3:T(2,128)(2,1)}, u32[]{:S(2)}, u32[]{:S(2)}) async-start(bf16[3,2,184,1152]{2,1,0,3:T(2,128)(2,1)} %pad_maximum_fusion.3), calls=%async_computation | async-start | bytes 7077888 | tf_op jit(solution)/shard_map/all_to_all | solution.py:117
  193.4 18.8 %all-to-all-start.1 = ((bf16[2,736,288]{2,0,1:T(2,128)(2,1)}), bf16[2,736,288]{2,0,1:T(2,128)(2,1)S(1)}, u32[]{:S(2)}, u32[]{:S(2)}) async-start(bf16[2,736,288]{2,0,1:T(2,128)(2,1)} %copy.85), calls=%async_computation.1 | async-start | bytes 2260992 | tf_op jit(solution)/shard_map/all_to_all | solution.py:129
  197.0 126.0 %reduce-scatter.13.cloned.1.call-start = ((), (), s32[]{:S(2)}) async-start(), calls=%async_computation.16 | async-start | bytes 6266880
  247.0 8.7 collective-permute-start
  264.3 119.7 %all-reduce.11.cloned.1.call-start = ((), (), s32[]{:S(2)}) async-start(), calls=%async_computation.12 | async-start | bytes 2506752 | tf_op jit(solution)/shard_map/psum | solution.py:55
  323.0 124.1 %all-gather.12.cloned.1.call-start = ((), (), s32[]{:S(2)}) async-start(), calls=%async_computation.11 | async-start | bytes 11280384 | tf_op jit(solution)/shard_map/all_gather | solution.py:43
  325.4 121.6 %copy-start.19 = (bf16[368,1152]{1,0:T(8,128)(2,1)S(1)}, bf16[368,1152]{1,0:T(8,128)(2,1)}, u32[]{:S(2)}) copy-start(bf16[368,1152]{1,0:T(8,128)(2,1)} %fusion.29) | copy-start | bytes 2543620
  325.5 250.9 %reduce-scatter.15.cloned.1.call-start = ((), (), s32[]{:S(2)}) async-start(), calls=%async_computation.17 | async-start | bytes 6266880
  386.9 81.9 %collective-permute-start.1 = (f32[1,144,4304]{2,1,0:T(8,128)}, f32[1,144,4304]{2,1,0:T(8,128)}, u32[]{:S(2)}, u32[]{:S(2)}) collective-permute-start(f32[1,144,4304]{2,1,0:T(8,128)} %convert_element_type.210), channel_id=1, source_target_pairs={{0,4},{4,0},{1,5},{5,1},{2,6},{6,2},{3,7},{7,3},{8,12},{12,8},{9,1... | collective-permute-start | bytes 7437320 | tf_op jit(solution)/shard_map/ppermute | solution.py:32
  499.6 8.5 collective-permute-start.2
  535.6 20.2 %all-to-all-start.2 = ((bf16[2,184,1152]{1,0,2:T(2,128)(2,1)}), bf16[2,184,1152]{1,0,2:T(2,128)(2,1)}, u32[]{:S(2)}, u32[]{:S(2)}) async-start(bf16[2,184,1152]{1,0,2:T(2,128)(2,1)} %copy.88), calls=%async_computation.2 | async-start | bytes 2359296 | tf_op jit(solution)/shard_map/all_to_all | solution.py:157
  539.9 97.6 %all-reduce.13.cloned.1.call-start = ((), (), s32[]{:S(2)}) async-start(), calls=%async_computation.13 | async-start | bytes 2506752 | tf_op jit(solution)/shard_map/psum | solution.py:55
  640.5 37.8 %collective-permute-start.3 = (f32[1,144,4304]{2,1,0:T(8,128)}, f32[1,144,4304]{2,1,0:T(8,128)}, u32[]{:S(2)}, u32[]{:S(2)}) collective-permute-start(f32[1,144,4304]{2,1,0:T(8,128)} %convert_element_type.215), channel_id=1, source_target_pairs={{0,4},{4,0},{1,5},{5,1},{2,6},{6,2},{3,7},{7,3},{8,12},{12,8},{9,1... | collective-permute-start | bytes 7437320 | tf_op jit(solution)/shard_map/ppermute | solution.py:32
  686.4 12.3 %collective-permute-start.4 = (bf16[4,144,1152]{2,1,0:T(8,128)(2,1)}, bf16[4,144,1152]{2,1,0:T(8,128)(2,1)}, u32[]{:S(2)}, u32[]{:S(2)}) collective-permute-start(bf16[4,144,1152]{2,1,0:T(8,128)(2,1)} %fusion.36), channel_id=1, source_target_pairs={{0,4},{4,0},{1,5},{5,1},{2,6},{6,2},{3,7},{7,3},{8,12},{12,8},{9,1... | collective-permute-start | bytes 3981320 | tf_op jit(solution)/shard_map/ppermute | solution.py:32
  694.0 44.3 %all-to-all-start.3 = ((bf16[3,2,736,288]{3,1,0,2:T(2,128)(2,1)}), bf16[3,2,736,288]{3,1,0,2:T(2,128)(2,1)}, u32[]{:S(2)}, u32[]{:S(2)}) async-start(bf16[3,2,736,288]{3,1,0,2:T(2,128)(2,1)} %pad_maximum_fusion.4), calls=%async_computation.3 | async-start | bytes 6782976 | tf_op jit(solution)/shard_map/all_to_all | solution.py:168
  698.7 73.2 %reduce-scatter.17.cloned.1.call-start = ((), (), s32[]{:S(2)}) async-start(), calls=%async_computation.18 | async-start | bytes 1658880
  702.3 105.5 %all-reduce.15.cloned.1.call-start = ((), (), s32[]{:S(2)}) async-start(), calls=%async_computation.14 | async-start | bytes 663552 | tf_op jit(solution)/shard_map/psum | solution.py:55
  772.0 114.5 %reduce-scatter.19.cloned.1.call-start = ((), (), s32[]{:S(2)}) async-start(), calls=%async_computation.19 | async-start | bytes 4976640
  808.8 6.6 collective-permute-start.5
  821.7 7.0 collective-permute-start.6
  834.9 104.4 %all-reduce.17.cloned.1.call-start = ((), (), s32[]{:S(2)}) async-start(), calls=%async_computation.15 | async-start | bytes 1990656 | tf_op jit(solution)/shard_map/psum | solution.py:55
  836.4 50.1 %copy-start.6 = (bf16[2,184,1152]{2,1,0:T(8,128)(2,1)S(1)}, bf16[2,184,1152]{2,1,0:T(8,128)(2,1)}, u32[]{:S(2)}) copy-start(bf16[2,184,1152]{2,1,0:T(8,128)(2,1)} %param.17) | copy-start | bytes 2543620
  836.4 50.0 %copy-start.26 = (f32[1152]{0:T(1024)S(1)}, f32[1152]{0:T(1024)}, u32[]{:S(2)}) copy-start(f32[1152]{0:T(1024)} %copy-done.25) | copy-start | bytes 13828
  836.4 50.0 %copy-start.31 = (f32[368]{0:T(512)S(1)}, f32[368]{0:T(512)}, u32[]{:S(2)}) copy-start(f32[368]{0:T(512)} %copy-done.30) | copy-start | bytes 4420
  836.5 50.0 %copy-start.33 = (f32[368]{0:T(512)S(1)}, f32[368]{0:T(512)}, u32[]{:S(2)}) copy-start(f32[368]{0:T(512)} %copy-done.32) | copy-start | bytes 4420
  942.0 55.0 %collective-permute-start.7 = (f32[1,144,3456]{2,1,0:T(8,128)}, f32[1,144,3456]{2,1,0:T(8,128)}, u32[]{:S(2)}, u32[]{:S(2)}) collective-permute-start(f32[1,144,3456]{2,1,0:T(8,128)} %convert_element_type.225), channel_id=1, source_target_pairs={{0,4},{4,0},{1,5},{5,1},{2,6},{6,2},{3,7},{7,3},{8,12},{12,8},{9,1... | collective-permute-start | bytes 5971976 | tf_op jit(solution)/shard_map/ppermute | solution.py:32
  943.6 50.2 %copy-start.4 = (f32[368,1152]{1,0:T(8,128)S(1)}, f32[368,1152]{1,0:T(8,128)}, u32[]{:S(2)}) copy-start(f32[368,1152]{1,0:T(8,128)} %copy-done.3) | copy-start | bytes 5087236
  943.6 50.2 %copy-start.9 = (bf16[2,184,1152]{2,1,0:T(8,128)(2,1)S(1)}, bf16[2,184,1152]{2,1,0:T(8,128)(2,1)}, u32[]{:S(2)}) copy-start(bf16[2,184,1152]{2,1,0:T(8,128)(2,1)} %param.33) | copy-start | bytes 2543620
  (41 other events, 348.9 us)
Sparse Core Ops, SparseCore 0:
  10.5 56.0 all-gather.5
  68.5 30.1 all-gather.7
  101.2 61.0 all-gather.9
  264.4 58.4 reduce-scatter.12
  325.2 58.7 all-reduce.10
  386.3 60.7 all-gather.11
  516.9 59.4 reduce-scatter.14
  578.7 58.7 all-reduce.12
  703.1 30.8 reduce-scatter.16
  772.1 35.6 all-reduce.14
  835.0 51.3 reduce-scatter.18
  888.7 50.6 all-reduce.16

commit v4 on v3

--- a/solution.py
+++ b/solution.py
@@ -139,6 +139,7 @@
     row_flag_rows = jnp.repeat(row_flags, part_rows)[:, None]
     output = (result * row_flag_rows).astype(bf16).reshape(pairs, part_rows, width)
 
+    out_grad, output = lax.optimization_barrier((out_grad, output))
     grad_rows = out_grad.reshape(pairs * part_rows, width).astype(f32) * row_flag_rows
     grad_low = grad_rows.astype(bf16)
     down_weight_grad_t = jnp.dot(grad_low.T, active_low, preferred_element_type=f32)

time: 1020 us -> 954 us (0.935)
  waiting for transfers between devices: 480 us -> 448 us
  local copies, waits for them, and re-layouts: 182 us -> 154 us
    all_gather x4, waiting for transfers between devices: 88.7 us -> 27.4 us  [gather_weight(): return lax.all_gather(piece, ('fsdp', 'core'), axis=0, tiled=True)]
    unnamed x16, waiting for transfers between devices: 97.9 us -> 116 us
  transfers between devices with their start and end apart: 24 -> 24, of which waited for: 16 -> 15; matrix products, arithmetic and copies ran while one was open for 31% -> 30% of each run, Pallas kernels for 0% -> 0%
where the time goes in v4:
time: 954 us; the launch traced here: 947 us
  waiting for transfers between devices  448 us (47%)
  local copies, waits for them, and re-layouts  154 us (16%)
  matrix products  150 us (16%)
  other arithmetic  95.5 us (10%)
  blocking collectives  63.5 us (7%)
  starting transfers between devices  19.8 us (2%)
  between operations  16 us (2%)
    psum x4, waiting for transfers between devices, reduce_weight(): part = lax.psum(part, ZAX).astype(jnp.float32)  180 us
    unnamed x16, waiting for transfers between devices  116 us
    all_to_all x1, waiting for transfers between devices, shards(): lax.all_to_all(qkv_tok, GROUP, split_axis=3, concat_axis=2, tiled=True)  41.1 us
    unnamed x2, blocking collectives  37.6 us
    all_to_all x1, waiting for transfers between devices, shards(): lax.all_to_all(dqkv, GROUP, split_axis=2, concat_axis=3, tiled=True)  36 us
    all_gather x4, waiting for transfers between devices, gather_weight(): return lax.all_gather(piece, ('fsdp', 'core'), axis=0, tiled=True)  27.4 us
    convert_element_type x4, other arithmetic, reduce_weight(): chip.astype(jnp.bfloat16)  26.9 us
    psum x1, blocking collectives, shards(): stacked = lax.psum(stacked, SEQ).reshape(-1)  25.9 us
  transfers between devices with their start and end apart: 24, of which 15 were waited for; matrix products, arithmetic and copies ran while one was open for 30% of the time, Pallas kernels for 0%

profile of v4, /device:TPU:0, one launch (start us, length us, event | category | flops | bytes accessed | tf_op | source)
XLA Modules:
  0.0 946.7 jit_solution(5881064450758406676)
XLA Ops:
  16.1 20.5 %all-reduce = f32[13520]{0:T(1024)S(1)} all-reduce(f32[13520]{0:T(1024)S(1)} %convert_dynamic-update-slice_fusion), channel_id=2, replica_groups=mesh['zh'=2,'zl'=2,'core'=2,'fsdp'=4] {'fsdp'}, use_global_device_ids=true, to_apply=%add | all-reduce | flops 13520 | bytes 108160
  39.5 27.4 %all-gather.6.cloned.1.call-done = bf16[1152,3456]{1,0:T(8,128)(2,1)} async-done(((bf16[144,3456]{1,0:T(8,128)(2,1)}), bf16[1152,3456]{1,0:T(8,128)(2,1)}) %all-gather.6.cloned.1.call-update) | async-done | bytes 7962640 | tf_op jit(solution)/shard_map/all_gather | solution.py:43
  84.4 8.1 pad_maximum_fusion.3
  98.0 41.1 %all-to-all-done = bf16[3,2,184,1152]{2,1,0,3:T(2,128)(2,1)} async-done(((bf16[3,2,184,1152]{2,1,0,3:T(2,128)(2,1)}), bf16[3,2,184,1152]{2,1,0,3:T(2,128)(2,1)}, u32[]{:S(2)}, u32[]{:S(2)}) %all-to-all-start) | async-done | bytes 2543648 | tf_op jit(solution)/shard_map/all_to_all | solution.py:117
  139.1 12.6 %copy.112 = bf16[3,2,184,4,288]{4,3,2,1,0:T(4,128)(2,1)} copy(bf16[3,2,184,4,288]{2,1,0,4,3:T(2,128)(2,1)} %bitcast.5) | data formatting | bytes 5087232 | tf_op jit(solution)/shard_map/all_to_all | solution.py:117
  169.7 10.9 %fusion.55 = (f32[2,4,736]{2,1,0:T(4,128)S(1)}, f32[2,4,736,736]{2,3,1,0:T(8,128)}) fusion(f32[2,736]{1,0:T(2,128)S(1)} %fusion.42, bf16[2,736,4,72]{1,3,2,0:T(8,128)(2,1)} %squeeze.70, bf16[2,736,4,72]{1,3,2,0:T(8,128)(2,1)S(1)} %squeeze.71), kind=kOutput, calls=%fused_computation.140 | convolution fusion | flops 641368768 | bytes 19059456 | tf_op jit(solution)/shard_map/sub | solution.py:124
  196.1 14.0 %all-to-all-done.1 = bf16[2,736,288]{2,0,1:T(2,128)(2,1)S(1)} async-done(((bf16[2,736,288]{2,0,1:T(2,128)(2,1)}), bf16[2,736,288]{2,0,1:T(2,128)(2,1)S(1)}, u32[]{:S(2)}, u32[]{:S(2)}) %all-to-all-start.1) | async-done | bytes 847904 | tf_op jit(solution)/shard_map/all_to_all | solution.py:129
  215.9 10.7 %convolution_add_fusion = f32[368,4304]{1,0:T(8,128)} fusion(bf16[1152,4304]{1,0:T(8,128)(2,1)} %all-gather.10.cloned.1.call-done, f32[4304]{0:T(1024)S(1)} %add.209, f32[368,1152]{1,0:T(8,128)S(1)} %get-tuple-element.84, f32[1152]{0:T(1024)S(1)} %add.206, f32[1152]{0:T(1024)S(1)} %mul.237, f32[368]{0:T(512)S(1)} %fusion.43, f32[368]{0:T(512)S(1)} %broadcast_multiply_fusion), kind=kOutput, calls=%fused_computation.22 | convolution fusion | flops 3652944640 | bytes 17977024 | tf_op jit(solution)/shard_map/dot_general | solution.py:135
  226.6 11.2 %fusion.25 = bf16[368,1152]{1,0:T(8,128)(2,1)} fusion(f32[368,1152]{1,0:T(8,128)S(1)} %get-tuple-element.84, bf16[1152,4304]{1,0:T(8,128)(2,1)} %all-gather.12.cloned.1.call-done, f32[368]{0:T(512)S(1)} %mul.246, f32[1152]{0:T(1024)S(1)} %add.215, f32[368,4304]{1,0:T(8,128)} %convolution_add_fusion), kind=kOutput, calls=%fused_computation.50 | convolution fusion | flops 3665191680 | bytes 18801600 | tf_op jit(solution)/shard_map/dot_general | solution.py:138
  241.2 11.8 %fusion.20 = f32[4,2,144,4304]{3,2,1,0:T(8,128)} fusion(bf16[4,2,144,368]{3,2,1,0:T(8,128)(2,1)} %bitcast.167, f32[368,4304]{1,0:T(8,128)} %convolution_add_fusion), kind=kOutput, calls=%fused_computation.43 | convolution fusion | flops 3663495936 | bytes 27016192 | tf_op jit(solution)/shard_map/dot_general | solution.py:145
  259.6 8.7 collective-permute-done
  268.3 8.6 fusion.3
  277.0 59.0 %reduce-scatter.13.cloned.1.call-done = bf16[1,144,4304]{2,1,0:T(8,128)(2,1)} async-done(((bf16[4,144,4304]{2,1,0:T(8,128)(2,1)}), bf16[1,144,4304]{2,1,0:T(8,128)(2,1)}) %reduce-scatter.13.cloned.1.call-update) | async-done | bytes 1239568
  336.3 60.8 %all-reduce.11.cloned.1.call-done = bf16[1,144,4304]{2,1,0:T(8,128)(2,1)} async-done(((bf16[1,144,4304]{2,1,0:T(8,128)(2,1)}), bf16[1,144,4304]{2,1,0:T(8,128)(2,1)}) %all-reduce.11.cloned.1.call-update) | async-done | bytes 1239568 | tf_op jit(solution)/shard_map/psum | solution.py:55
  398.6 12.0 %convert_reduce_fusion = (f32[4304]{0:T(1024)S(1)}, bf16[368,4304]{1,0:T(8,128)(2,1)S(1)}) fusion(f32[368,4304]{1,0:T(8,128)} %convolution_add_fusion, bf16[368,1152]{1,0:T(8,128)(2,1)} %fusion.29, bf16[1152,4304]{1,0:T(8,128)(2,1)} %all-gather.12.cloned.1.call-done), kind=kOutput, calls=%fused_computation.29 | convolution fusion | flops 3690417408 | bytes 20284736 | tf_op jit(solution)/shard_map/dot_general | solution.py:147
  410.7 9.9 %fusion.46 = f32[1152,4304]{0,1:T(8,128)} fusion(bf16[368,4304]{1,0:T(8,128)(2,1)S(1)} %get-tuple-element.48, f32[368,1152]{1,0:T(8,128)S(1)} %get-tuple-element.84, f32[1152]{0:T(1024)S(1)} %add.206, f32[1152]{0:T(1024)S(1)} %mul.237, f32[368]{0:T(512)S(1)} %fusion.43, f32[368]{0:T(512)S(1)} %broadcast_multiply_fusion), kind=kOutput, calls=%fused_computation.133 | convolution fusion | flops 3651360768 | bytes 24708480 | tf_op jit(solution)/shard_map/dot_general | solution.py:149
  423.6 22.0 %copy.104 = f32[1152,4304]{1,0:T(8,128)} copy(f32[1152,4304]{0,1:T(8,128)} %fusion.46) | data formatting | bytes 39665664 | tf_op jit(solution)/shard_map/optimization_barrier | solution.py:194
  458.6 8.6 fusion.2
  467.2 9.3 multiply_reduce_fusion.2
  494.9 10.5 %all-to-all-done.2 = bf16[2,184,1152]{1,0,2:T(2,128)(2,1)S(1)} async-done(((bf16[2,184,1152]{1,0,2:T(2,128)(2,1)}), bf16[2,184,1152]{1,0,2:T(2,128)(2,1)S(1)}, u32[]{:S(2)}, u32[]{:S(2)}) %all-to-all-start.2) | async-done | bytes 847904 | tf_op jit(solution)/shard_map/all_to_all | solution.py:158
  507.3 13.0 %multiply_reduce_fusion = (f32[2,4,736]{2,1,0:T(4,128)S(1)}, f32[2,4,736,736]{2,3,1,0:T(8,128)}) fusion(f32[2,4,736,736]{2,3,1,0:T(8,128)} %get-tuple-element.82, f32[2,4,736]{2,1,0:T(4,128)S(1)} %get-tuple-element.81, bf16[2,736,4,72]{1,3,2,0:T(8,128)(2,1)S(1)} %reshape.263, bf16[2,736,4,72]{1,3,2,0:T(8,128)(2,1)} %squeeze.69), kind=kOutput, calls=%fused_computation.2 | convolution fusion | flops 637028608 | bytes 36411392 | tf_op jit(solution)/shard_map/pqhd,pkhd->phqk/dot_general | solution.py:162
  526.4 16.4 %multiply_convert_fusion = bf16[2,4,736,736]{2,3,1,0:T(8,128)(2,1)} fusion(f32[2,4,736,736]{2,3,1,0:T(8,128)} %get-tuple-element.87, f32[2,4,736]{2,1,0:T(4,128)S(1)} %get-tuple-element.86, f32[2,4,736,736]{2,3,1,0:T(8,128)} %get-tuple-element.82, f32[2,4,736]{2,1,0:T(4,128)S(1)} %get-tuple-element.81), kind=kLoop, calls=%fused_computation.1 | loop fusion | flops 17334272 | bytes 43382784 | tf_op jit(solution)/shard_map/convert_element_type | solution.py:164
  542.8 44.8 %all-reduce.13.cloned.1.call-done = bf16[1,144,4304]{2,1,0:T(8,128)(2,1)} async-done(((bf16[1,144,4304]{2,1,0:T(8,128)(2,1)}), bf16[1,144,4304]{2,1,0:T(8,128)(2,1)}) %all-reduce.13.cloned.1.call-update) | async-done | bytes 1239568 | tf_op jit(solution)/shard_map/psum | solution.py:55
  590.5 8.9 fusion.33
  643.4 36.0 %all-to-all-done.3 = bf16[3,2,736,288]{3,1,0,2:T(2,128)(2,1)} async-done(((bf16[3,2,736,288]{3,1,0,2:T(2,128)(2,1)}), bf16[3,2,736,288]{3,1,0,2:T(2,128)(2,1)}, u32[]{:S(2)}, u32[]{:S(2)}) %all-to-all-start.3) | async-done | bytes 2543648 | tf_op jit(solution)/shard_map/all_to_all | solution.py:169
  679.4 13.1 %copy.117 = bf16[3,2,4,184,288]{3,2,4,1,0:T(4,128)(2,1)} copy(bf16[3,2,4,184,288]{4,1,0,3,2:T(2,128)(2,1)} %bitcast.26) | data formatting | bytes 5087232 | tf_op jit(solution)/shard_map/all_to_all | solution.py:169
  715.1 30.9 %all-reduce.15.cloned.1.call-done = bf16[1,144,1152]{2,1,0:T(8,128)(2,1)} async-done(((bf16[1,144,1152]{2,1,0:T(8,128)(2,1)}), bf16[1,144,1152]{2,1,0:T(8,128)(2,1)}) %all-reduce.15.cloned.1.call-update) | async-done | bytes 331792 | tf_op jit(solution)/shard_map/psum | solution.py:55
  773.9 50.4 %reduce-scatter.19.cloned.1.call-done = bf16[1,144,3456]{2,1,0:T(8,128)(2,1)} async-done(((bf16[4,144,3456]{2,1,0:T(8,128)(2,1)}), bf16[1,144,3456]{2,1,0:T(8,128)(2,1)}) %reduce-scatter.19.cloned.1.call-update) | async-done | bytes 995344
  824.4 9.3 fusion.47
  833.7 43.5 %all-reduce.17.cloned.1.call-done = bf16[1,144,3456]{2,1,0:T(8,128)(2,1)} async-done(((bf16[1,144,3456]{2,1,0:T(8,128)(2,1)}), bf16[1,144,3456]{2,1,0:T(8,128)(2,1)}) %all-reduce.17.cloned.1.call-update) | async-done | bytes 995344 | tf_op jit(solution)/shard_map/psum | solution.py:55
  886.8 17.1 %all-reduce.1 = f32[4,3380]{1,0:T(4,128)S(1)} all-reduce(f32[4,3380]{1,0:T(4,128)S(1)} %concatenate.26), channel_id=3, replica_groups=mesh['zh'=2,'zl'=2,'core'=2,'fsdp'=4] {'fsdp'}, use_global_device_ids=true, to_apply=%region_20.21.clone | all-reduce | flops 13520 | bytes 108160
  904.5 25.9 %psum.35 = f32[1,3380]{1,0:T(1,128)S(1)} all-reduce(f32[1,3380]{1,0:T(1,128)S(1)} %constant_dynamic-slice_fusion.5), channel_id=1, replica_groups=mesh['zh'=2,'zl'=2,'core'=2,'fsdp'=4] {'zh','zl','core'}, use_global_device_ids=true, to_apply=%region_21.22 | all-reduce | flops 3380 | bytes 27040 | tf_op jit(solution)/shard_map/psum | solution.py:184
  (267 shorter events, 243.6 us)
Async XLA Ops:
  7.2 59.7 %all-gather.6.cloned.1.call-start = ((), (), s32[]{:S(2)}) async-start(), calls=%async_computation.8 | async-start | bytes 8957952 | tf_op jit(solution)/shard_map/all_gather | solution.py:43
  9.7 202.4 %all-gather.8.cloned.1.call-start = ((), (), s32[]{:S(2)}) async-start(), calls=%async_computation.9 | async-start | bytes 2985984 | tf_op jit(solution)/shard_map/all_gather | solution.py:43
  10.6 205.4 %all-gather.10.cloned.1.call-start = ((), (), s32[]{:S(2)}) async-start(), calls=%async_computation.10 | async-start | bytes 11280384 | tf_op jit(solution)/shard_map/all_gather | solution.py:43
  11.9 214.8 %all-gather.12.cloned.1.call-start = ((), (), s32[]{:S(2)}) async-start(), calls=%async_computation.11 | async-start | bytes 11280384 | tf_op jit(solution)/shard_map/all_gather | solution.py:43
  37.0 35.9 %copy-start.29 = (f32[368]{0:T(512)}, f32[368]{0:T(512)S(1)}, u32[]{:S(2)}) copy-start(f32[368]{0:T(512)S(1)} %div.47) | copy-start | bytes 4420
  37.3 35.7 %copy-start.25 = (f32[1152]{0:T(1024)}, f32[1152]{0:T(1024)S(1)}, u32[]{:S(2)}) copy-start(f32[1152]{0:T(1024)S(1)} %mul.225) | copy-start | bytes 13828
  37.8 35.2 %copy-start.31 = (f32[368]{0:T(512)}, f32[368]{0:T(512)S(1)}, u32[]{:S(2)}) copy-start(f32[368]{0:T(512)S(1)} %rsqrt.20) | copy-start | bytes 4420
  92.5 46.5 %all-to-all-start = ((bf16[3,2,184,1152]{2,1,0,3:T(2,128)(2,1)}), bf16[3,2,184,1152]{2,1,0,3:T(2,128)(2,1)}, u32[]{:S(2)}, u32[]{:S(2)}) async-start(bf16[3,2,184,1152]{2,1,0,3:T(2,128)(2,1)} %pad_maximum_fusion.3), calls=%async_computation | async-start | bytes 7077888 | tf_op jit(solution)/shard_map/all_to_all | solution.py:117
  191.2 18.8 %all-to-all-start.1 = ((bf16[2,736,288]{2,0,1:T(2,128)(2,1)}), bf16[2,736,288]{2,0,1:T(2,128)(2,1)S(1)}, u32[]{:S(2)}, u32[]{:S(2)}) async-start(bf16[2,736,288]{2,0,1:T(2,128)(2,1)} %copy.85), calls=%async_computation.1 | async-start | bytes 2260992 | tf_op jit(solution)/shard_map/all_to_all | solution.py:129
  194.7 141.3 %reduce-scatter.13.cloned.1.call-start = ((), (), s32[]{:S(2)}) async-start(), calls=%async_computation.16 | async-start | bytes 6266880
  259.6 8.7 collective-permute-start
  276.9 120.1 %all-reduce.11.cloned.1.call-start = ((), (), s32[]{:S(2)}) async-start(), calls=%async_computation.12 | async-start | bytes 2506752 | tf_op jit(solution)/shard_map/psum | solution.py:55
  336.1 190.3 %reduce-scatter.15.cloned.1.call-start = ((), (), s32[]{:S(2)}) async-start(), calls=%async_computation.17 | async-start | bytes 6266880
  398.6 22.1 %collective-permute-start.1 = (f32[1,144,4304]{2,1,0:T(8,128)S(1)}, f32[1,144,4304]{2,1,0:T(8,128)S(1)}, u32[]{:S(2)}, u32[]{:S(2)}) collective-permute-start(f32[1,144,4304]{2,1,0:T(8,128)S(1)} %convert_element_type.210), channel_id=1, source_target_pairs={{0,4},{4,0},{1,5},{5,1},{2,6},{6,2},{3,7},{7,3},{8,12},{12,8},{9,1... | collective-permute-start | bytes 7437320 | tf_op jit(solution)/shard_map/ppermute | solution.py:32
  449.9 8.6 collective-permute-start.2
  486.1 19.3 %all-to-all-start.2 = ((bf16[2,184,1152]{1,0,2:T(2,128)(2,1)}), bf16[2,184,1152]{1,0,2:T(2,128)(2,1)S(1)}, u32[]{:S(2)}, u32[]{:S(2)}) async-start(bf16[2,184,1152]{1,0,2:T(2,128)(2,1)} %copy.88), calls=%async_computation.2 | async-start | bytes 2359296 | tf_op jit(solution)/shard_map/all_to_all | solution.py:158
  489.6 98.0 %all-reduce.13.cloned.1.call-start = ((), (), s32[]{:S(2)}) async-start(), calls=%async_computation.13 | async-start | bytes 2506752 | tf_op jit(solution)/shard_map/psum | solution.py:55
  590.5 28.9 %collective-permute-start.3 = (f32[1,144,4304]{2,1,0:T(8,128)}, f32[1,144,4304]{2,1,0:T(8,128)}, u32[]{:S(2)}, u32[]{:S(2)}) collective-permute-start(f32[1,144,4304]{2,1,0:T(8,128)} %convert_element_type.215), channel_id=1, source_target_pairs={{0,4},{4,0},{1,5},{5,1},{2,6},{6,2},{3,7},{7,3},{8,12},{12,8},{9,1... | collective-permute-start | bytes 7437320 | tf_op jit(solution)/shard_map/ppermute | solution.py:32
  627.5 12.3 %collective-permute-start.4 = (bf16[4,144,1152]{2,1,0:T(8,128)(2,1)}, bf16[4,144,1152]{2,1,0:T(8,128)(2,1)}, u32[]{:S(2)}, u32[]{:S(2)}) collective-permute-start(bf16[4,144,1152]{2,1,0:T(8,128)(2,1)} %fusion.36), channel_id=1, source_target_pairs={{0,4},{4,0},{1,5},{5,1},{2,6},{6,2},{3,7},{7,3},{8,12},{12,8},{9,1... | collective-permute-start | bytes 3981320 | tf_op jit(solution)/shard_map/ppermute | solution.py:32
  635.0 44.3 %all-to-all-start.3 = ((bf16[3,2,736,288]{3,1,0,2:T(2,128)(2,1)}), bf16[3,2,736,288]{3,1,0,2:T(2,128)(2,1)}, u32[]{:S(2)}, u32[]{:S(2)}) async-start(bf16[3,2,736,288]{3,1,0,2:T(2,128)(2,1)} %pad_maximum_fusion.4), calls=%async_computation.3 | async-start | bytes 6782976 | tf_op jit(solution)/shard_map/all_to_all | solution.py:169
  639.8 70.4 %reduce-scatter.17.cloned.1.call-start = ((), (), s32[]{:S(2)}) async-start(), calls=%async_computation.18 | async-start | bytes 1658880
  643.3 102.7 %all-reduce.15.cloned.1.call-start = ((), (), s32[]{:S(2)}) async-start(), calls=%async_computation.14 | async-start | bytes 663552 | tf_op jit(solution)/shard_map/psum | solution.py:55
  710.1 114.2 %reduce-scatter.19.cloned.1.call-start = ((), (), s32[]{:S(2)}) async-start(), calls=%async_computation.19 | async-start | bytes 4976640
  747.0 6.3 collective-permute-start.5
  759.6 7.0 collective-permute-start.6
  772.8 51.6 %copy-start.6 = (bf16[2,184,1152]{2,1,0:T(8,128)(2,1)S(1)}, bf16[2,184,1152]{2,1,0:T(8,128)(2,1)}, u32[]{:S(2)}) copy-start(bf16[2,184,1152]{2,1,0:T(8,128)(2,1)} %param.17) | copy-start | bytes 2543620
  772.8 51.6 %copy-start.26 = (f32[1152]{0:T(1024)S(1)}, f32[1152]{0:T(1024)}, u32[]{:S(2)}) copy-start(f32[1152]{0:T(1024)} %copy-done.25) | copy-start | bytes 13828
  772.8 51.6 %copy-start.30 = (f32[368]{0:T(512)S(1)}, f32[368]{0:T(512)}, u32[]{:S(2)}) copy-start(f32[368]{0:T(512)} %copy-done.29) | copy-start | bytes 4420
  772.8 51.6 %copy-start.32 = (f32[368]{0:T(512)S(1)}, f32[368]{0:T(512)}, u32[]{:S(2)}) copy-start(f32[368]{0:T(512)} %copy-done.31) | copy-start | bytes 4420
  772.8 104.4 %all-reduce.17.cloned.1.call-start = ((), (), s32[]{:S(2)}) async-start(), calls=%async_computation.15 | async-start | bytes 1990656 | tf_op jit(solution)/shard_map/psum | solution.py:55
  880.0 55.0 %collective-permute-start.7 = (f32[1,144,3456]{2,1,0:T(8,128)}, f32[1,144,3456]{2,1,0:T(8,128)}, u32[]{:S(2)}, u32[]{:S(2)}) collective-permute-start(f32[1,144,3456]{2,1,0:T(8,128)} %convert_element_type.225), channel_id=1, source_target_pairs={{0,4},{4,0},{1,5},{5,1},{2,6},{6,2},{3,7},{7,3},{8,12},{12,8},{9,1... | collective-permute-start | bytes 5971976 | tf_op jit(solution)/shard_map/ppermute | solution.py:32
  881.6 50.2 %copy-start.4 = (f32[368,1152]{1,0:T(8,128)S(1)}, f32[368,1152]{1,0:T(8,128)}, u32[]{:S(2)}) copy-start(f32[368,1152]{1,0:T(8,128)} %copy-done.3) | copy-start | bytes 5087236
  (40 other events, 301.4 us)
Sparse Core Ops, SparseCore 0:
  10.5 56.4 all-gather.5
  68.8 30.1 all-gather.7
  101.4 61.1 all-gather.9
  165.0 61.2 all-gather.11
  277.1 58.9 reduce-scatter.12
  338.3 58.7 all-reduce.10
  467.4 58.9 reduce-scatter.14
  528.8 58.7 all-reduce.12
  644.2 30.8 reduce-scatter.16
  710.3 35.6 all-reduce.14
  772.9 51.3 reduce-scatter.18
  826.6 50.6 all-reduce.16
